TPU v7x, 128 devices: a whole 4x4x4 slice. The times are simulated.
128 devices in a mesh: grp: 4 (over x_hi, core), tile: 32 (over z, y, x_lo).
Axes of the slice: x: 4 (x_hi: 2, x_lo: 2; x = x_hi * 2 + x_lo), y: 4, z: 4, core: 2. Of those that a mesh axis runs over, the one named last changes fastest.
Arguments:
- factors: bfloat16 [4096, 128, 128], P('tile', 'grp'), may hold values from -0.09375 to 0.09375
- amplitudes: bfloat16 [2048, 128, 128], P('tile', 'grp'), may hold values from -6 to 6
- tile_mask: int32 [32, 2, 2], replicated, may hold values 0 or 1
Outputs:
- residual: bfloat16 [128, 64, 2048], P('tile', None, 'grp')
All inputs are finite; a program needn't handle non-finite values.
Results may differ from a plain program's by a relative error of at most 0.011.
Values may be sent and summed in bfloat16 or wider, within the bound.
A program may use at most 128 MiB of HBM per device.

v0:
```python
import jax
import jax.numpy as jnp
from jax import lax
from jax.sharding import PartitionSpec as P

VB = 64
NB = 64
IJB = 64


def in_blocks(value, dim, peers):
    lengths = value.shape
    tiles = value.reshape(*lengths[:dim], peers, lengths[dim] // peers, *lengths[dim + 1 :])
    return jnp.moveaxis(tiles, dim, 0)


def sent_and_summed(value, axis, dim):
    peers = lax.axis_size(axis)
    tiles = lax.all_to_all(in_blocks(value, dim, peers), axis, 0, 0, tiled=True)
    return jnp.sum(tiles.astype(jnp.float32), axis=0)


def on_device(factors, amplitudes, tile_mask):
    aux_local, d_quarter, virtuals = factors.shape
    tiles = lax.axis_size("tile")
    groups = lax.axis_size("grp")
    tile_index = lax.axis_index("tile")
    group_index = lax.axis_index("grp")
    a_local = virtuals // tiles
    row_local = amplitudes.shape[0]
    pairs = row_local * tiles
    pair_quarter = pairs // groups
    window = factors[:, :, :NB]
    window_all = lax.all_gather(window, "tile", axis=0, tiled=True)
    window_matrix = window_all.reshape(aux_local * tiles, d_quarter * NB)
    swapped = lax.all_to_all(factors, "tile", split_axis=2, concat_axis=0, tiled=True)
    rows_full = lax.all_gather(swapped, "grp", axis=1, tiled=True)
    left_matrix = rows_full.reshape(aux_local * tiles, virtuals * a_local)
    gram = lax.dot_general(
        left_matrix, window_matrix, (((0,), (0,)), ((), ())), preferred_element_type=jnp.float32
    )
    integrals = (
        gram.astype(jnp.bfloat16).reshape(virtuals, a_local, d_quarter, NB).transpose(2, 0, 1, 3)
    )
    integrals = integrals.reshape(d_quarter * virtuals, a_local * NB)
    pair_rows = tile_index * row_local + jnp.arange(row_local, dtype=jnp.int32)
    c_blocks = jnp.arange(virtuals, dtype=jnp.int32) // VB
    d_blocks = (group_index * d_quarter + jnp.arange(d_quarter, dtype=jnp.int32)) // VB
    amp_mask = tile_mask[pair_rows // IJB][:, c_blocks][:, :, d_blocks].transpose(0, 2, 1)
    screened = amplitudes * amp_mask.astype(jnp.bfloat16)
    piece = lax.all_gather(screened, "tile", axis=0, tiled=True)
    flat = piece.reshape(piece.shape[0], d_quarter * virtuals)
    partials = lax.dot_general(
        integrals, flat, (((0,), (1,)), ((), ())), preferred_element_type=jnp.float32
    )
    summed = sent_and_summed(partials.astype(jnp.bfloat16), "grp", 1)
    out_rows = group_index * pair_quarter + jnp.arange(pair_quarter, dtype=jnp.int32)
    a_blocks = (tile_index * a_local + jnp.arange(a_local, dtype=jnp.int32)) // VB
    b_blocks = jnp.arange(NB, dtype=jnp.int32) // VB
    res_mask = tile_mask[out_rows // IJB][:, a_blocks][:, :, b_blocks].transpose(1, 2, 0)
    result = summed.reshape(a_local, NB, pair_quarter) * res_mask.astype(jnp.float32)
    return result.astype(jnp.bfloat16)


def solution(mesh):
    placed = (P("tile", "grp", None), P("tile", "grp", None), P())
    return jax.shard_map(
        on_device, mesh=mesh, in_specs=placed, out_specs=P("tile", None, "grp"), check_vma=False
    )
```

profile of v0, /device:TPU:1, one launch (start us, length us, event | category | flops | bytes accessed | tf_op | source)
XLA Modules:
  0.0 861.4 jit_solution(1061874892927342770)
XLA Ops:
  6.5 2.6 copy.48
  9.1 26.4 %all_to_all.23 = bf16[128,32,128]{0,1,2:T(8,128)(2,1)S(1)} all-to-all(bf16[128,32,128]{0,1,2:T(8,128)(2,1)S(1)} %copy.48), channel_id=1, replica_groups=mesh['grp'=4,'tile'=32] {'tile'}, dimensions={2} | all-to-all | bytes 2097152 | tf_op jit(solution)/shard_map/all_to_all | solution.py:36
  35.5 1.2 copy.77
  36.8 1.9 copy.63
  38.9 0.7 gather_fusion
  39.7 0.7 gather_fusion.1
  40.6 0.6 gather_fusion.2
  41.6 1.0 bitcast_multiply_fusion.1
  42.7 31.7 %all-gather.4.cloned.1.call-done = bf16[4096,128,4]{0,1,2:T(8,128)(2,1)} async-done(((bf16[4096,32,4]{0,1,2:T(8,128)(2,1)}), bf16[4096,128,4]{0,1,2:T(8,128)(2,1)}) %all-gather.4.cloned.1.call-update) | async-done | bytes 4194320 | tf_op jit(solution)/shard_map/all_gather | solution.py:37
  74.3 7.4 copy.50
  81.7 6.9 reshape.351
  88.7 345.4 %all-gather.6.cloned.1.call-done = bf16[4096,32,64]{0,2,1:T(8,128)(2,1)} async-done(((bf16[128,32,64]{0,2,1:T(8,128)(2,1)}), bf16[4096,32,64]{0,2,1:T(8,128)(2,1)}) %all-gather.6.cloned.1.call-update) | async-done | bytes 16777232 | tf_op jit(solution)/shard_map/all_gather | solution.py:34
  434.1 13.6 %convolution_convert_fusion = bf16[512,2048]{1,0:T(8,128)(2,1)S(1)} fusion(bf16[4096,512]{0,1:T(8,128)(2,1)} %reshape.351, bf16[4096,2048]{0,1:T(8,128)(2,1)} %bitcast.61), kind=kOutput, calls=%fused_computation.6 | convolution fusion | flops 8590983168 | bytes 23068672 | tf_op jit(solution)/shard_map/dot_general | solution.py:39
  447.7 5.4 reshape.353
  453.1 7.8 copy.52
  460.9 339.4 %all-gather.8.cloned.1.call-done = bf16[2048,32,128]{2,0,1:T(8,128)(2,1)} async-done(((bf16[64,32,128]{2,0,1:T(8,128)(2,1)}), bf16[2048,32,128]{2,0,1:T(8,128)(2,1)}) %all-gather.8.cloned.1.call-update) | async-done | bytes 16777232 | tf_op jit(solution)/shard_map/all_gather | solution.py:51
  800.2 22.6 %copy.57 = bf16[2048,32,128]{0,2,1:T(8,128)(2,1)} copy(bf16[2048,32,128]{2,0,1:T(8,128)(2,1)} %all-gather.8.cloned.1.call-done) | data formatting | bytes 33554432 | tf_op jit(solution)/shard_map/all_gather | solution.py:51
  822.9 9.8 %convolution_convert_fusion.1 = bf16[256,2048]{1,0:T(8,128)(2,1)S(1)} fusion(bf16[2048,4096]{0,1:T(8,128)(2,1)} %bitcast.53, bf16[32,8,32,128]{3,2,1,0:T(8,128)(2,1)S(1)} %bitcast.57), kind=kOutput, calls=%fused_computation.7 | convolution fusion | flops 4295491584 | bytes 19922944 | tf_op jit(solution)/shard_map/dot_general | solution.py:53
  832.7 1.1 copy.78
  833.7 5.1 all-to-all-start.1
  838.9 2.1 gather_fusion.3
  841.8 0.9 gather_fusion.5
  842.7 11.1 %all-to-all-done.1 = bf16[4,256,512]{2,1,0:T(8,128)(2,1)S(1)} async-done(((bf16[4,256,512]{2,1,0:T(8,128)(2,1)}), bf16[4,256,512]{2,1,0:T(8,128)(2,1)S(1)}, u32[]{:S(2)}, u32[]{:S(2)}) %all-to-all-start.1) | async-done | bytes 1048608 | tf_op jit(solution)/shard_map/all_to_all | solution.py:19
  854.0 0.9 fusion.2
  (31 shorter events, 1.9 us)
Async XLA Ops:
  6.5 30.3 %copy-start = (bf16[128,32,128]{2,1,0:T(8,128)(2,1)S(1)}, bf16[128,32,128]{2,1,0:T(8,128)(2,1)}, u32[]{:S(2)}) copy-start(bf16[128,32,128]{2,1,0:T(8,128)(2,1)} %param.3) | copy-start | bytes 3145732
  6.5 67.8 %all-gather.4.cloned.1.call-start = ((), (), s32[]{:S(2)}) async-start(), calls=%async_computation.2 | async-start | bytes 5242880 | tf_op jit(solution)/shard_map/all_gather | solution.py:37
  9.1 29.7 %copy-start.2 = (s32[32,2,2]{0,2,1:T(2,128)S(1)}, s32[32,2,2]{0,2,1:T(2,128)}, u32[]{:S(2)}) copy-start(s32[32,2,2]{0,2,1:T(2,128)} %param.5) | copy-start | bytes 1540
  36.8 397.3 %all-gather.6.cloned.1.call-start = ((), (), s32[]{:S(2)}) async-start(), calls=%async_computation.3 | async-start | bytes 17301504 | tf_op jit(solution)/shard_map/all_gather | solution.py:34
  38.7 761.5 %all-gather.8.cloned.1.call-start = ((), (), s32[]{:S(2)}) async-start(), calls=%async_computation.4 | async-start | bytes 17301504 | tf_op jit(solution)/shard_map/all_gather | solution.py:51
  40.6 1.0 copy-start.1
  833.7 20.1 %all-to-all-start.1 = ((bf16[4,256,512]{2,1,0:T(8,128)(2,1)}), bf16[4,256,512]{2,1,0:T(8,128)(2,1)S(1)}, u32[]{:S(2)}, u32[]{:S(2)}) async-start(bf16[4,256,512]{2,1,0:T(8,128)(2,1)} %bitcast.48), calls=%async_computation.1 | async-start | bytes 2097152 | tf_op jit(solution)/shard_map/all_to_all | solution.py:19
Sparse Core Ops, SparseCore 0:
  36.9 37.3 all-gather.3
  75.9 358.1 all-gather.5
  435.7 364.4 all-gather.7
where the time goes:
time: 862 us; the launch traced here: 861 us
  waiting for transfers between devices  728 us (84%)
  local copies, waits for them, and re-layouts  63.3 us (7%)
  blocking collectives  26.4 us (3%)
  matrix products  23.4 us (3%)
  between operations  13.3 us (2%)
    all_gather x1, waiting for transfers between devices, on_device(): window_all = lax.all_gather(window, 'tile', axis=0, tiled=True)  345 us
    all_gather x1, waiting for transfers between devices, on_device(): piece = lax.all_gather(screened, 'tile', axis=0, tiled=True)  339 us
    all_gather x1, waiting for transfers between devices, on_device(): rows_full = lax.all_gather(swapped, 'grp', axis=1, tiled=True)  31.7 us
    all_to_all x1, blocking collectives, on_device(): lax.all_to_all(factors, 'tile', split_axis=2, concat_axis=0, tiled=True)  26.4 us
    all_gather x1, local copies, waits for them, and re-layouts, on_device(): piece = lax.all_gather(screened, 'tile', axis=0, tiled=True)  22.6 us
  transfers between devices with their start and end apart: 4, of which 4 were waited for; matrix products, arithmetic and copies ran while one was open for 6% of the time, Pallas kernels for 0%

commit v1 on v0

v1 whole, which is shorter than its diff:
```python
import functools

import jax
import jax.numpy as jnp
from jax import lax
from jax.experimental import pallas as pl
from jax.experimental.pallas import tpu as pltpu
from jax.sharding import PartitionSpec as P

MESH = pl.DeviceIdType.MESH
NB = 64
BF = jnp.bfloat16
F32 = jnp.float32


def remote(src, dst, send, recv, dev):
    return pltpu.make_async_remote_copy(
        src_ref=src, dst_ref=dst, send_sem=send, recv_sem=recv, device_id=dev, device_id_type=MESH
    )


class Gather:
    EVENTS = 18

    def __init__(self, piece, i, j, up, down, pair, send, recv, sibling=None):
        self.piece, self.i, self.j = piece, i, j
        self.up, self.down, self.pair = up, down, pair
        self.send, self.recv = send, recv
        self.sibling = sibling
        self.sent = []
        i1, i2, i3, o = lax.rem(i + 1, 4), lax.rem(i + 2, 4), lax.rem(i + 3, 4), 1 - j
        self.brings = [
            (i3, j, 0, None), (i1, j, 0, None), (i2, j, 0, 0), (i2, j, 0, 1),
            (i, o, 0, None), (i3, o, 0, None), (i1, o, 0, None), (i2, o, 0, 0), (i2, o, 0, 1),
            (i, o, 1, None),
            (i3, j, 1, None), (i1, j, 1, None), (i3, o, 1, None), (i1, o, 1, None),
            (i2, j, 1, 0), (i2, j, 1, 1), (i2, o, 1, 0), (i2, o, 1, 1),
        ]
        self.sends = [
            ((i, j, 0, None), up), ((i, j, 0, None), down), ((i3, j, 0, 0), up), ((i1, j, 0, 1), down),
            ((i, j, 0, None), pair), ((i3, j, 0, None), pair), ((i1, j, 0, None), pair), ((i2, j, 0, 0), pair), ((i2, j, 0, 1), pair),
            ((i, j, 1, None), pair),
            ((i, j, 1, None), up), ((i, j, 1, None), down), ((i, o, 1, None), up), ((i, o, 1, None), down),
            ((i3, j, 1, 0), up), ((i1, j, 1, 1), down), ((i3, o, 1, 0), up), ((i1, o, 1, 1), down),
        ]
        self.then = {0: (2, 5), 1: (3, 6), 2: (7,), 3: (8,), 9: (12, 13), 10: (14,), 11: (15,), 12: (16,), 13: (17,)}

    def _go(self, e):
        where, dev = self.sends[e]
        ref = self.piece(*where)
        copy = remote(ref, ref, self.send.at[e], self.recv.at[e], dev)
        copy.start()
        self.sent.append(copy)

    def _share(self, slot, where):
        if self.sibling is not None:
            dev, send, recv = self.sibling
            ref = self.piece(*where)
            copy = remote(ref, ref, send.at[slot], recv.at[slot], dev)
            copy.start()
            self.sent.append(copy)

    def begin(self, order=(9, 0, 1, 4, 10, 11)):
        for e in order:
            self._go(e)
        self._share(18, (self.i, self.j, 0, None))
        self._share(19, (self.i, self.j, 1, None))

    def event(self, e):
        ref = self.piece(*self.brings[e])
        remote(ref, ref, self.send.at[e], self.recv.at[e], self.pair).wait_recv()
        for s in self.then.get(e, ()):
            self._go(s)
        self._share(e, self.brings[e])

    def sibling_wait(self, other_piece):
        dev, send, recv = self.sibling
        for slot in range(20):
            where = self.brings[slot] if slot < 18 else (self.i, self.j, slot - 18, None)
            ref = other_piece(*where)
            remote(ref, ref, send.at[slot], recv.at[slot], dev).wait_recv()

    def finish(self):
        for copy in self.sent:
            copy.wait_send()


def kernel(
    fl, fr, tt, out,
    lb, rb, tb, gr, w, pb, rs,
    la_s, la_r, ra_s, ra_r, ta_s, ta_r,
    lg_s, lg_r, rg_s, rg_r, tg_s, tg_r,
    rd_s, rd_r, td_s, td_r, rs_s, rs_r,
):
    g, t = lax.axis_index("grp"), lax.axis_index("tile")
    xh, k = g // 2, lax.rem(g, 2)
    z, y, xl = t // 8, lax.rem(t // 2, 4), lax.rem(t, 2)
    v = lax.rem(xl + xh, 2)

    def dev(xh_, k_, z_, y_, xl_):
        return {"grp": xh_ * 2 + k_, "tile": z_ * 8 + y_ * 2 + xl_}

    yhi, ylo = y // 2, lax.rem(y, 2)
    routed = []
    for src, dst, ss, rr in ((fr, rb, ra_s, ra_r), (tt, tb, ta_s, ta_r)):
        for dl in range(2):
            y_to = 2 * k + dl

            @pl.when(y_to == y)
            def _():
                pltpu.make_async_copy(src.at[dl], dst.at[z, xl, y], rr.at[ylo]).start()

            @pl.when(y_to != y)
            def _():
                remote(src.at[dl], dst.at[z, xl, y], ss.at[dl], rr.at[ylo], dev(xh, yhi, z, y_to, xl)).start()

            routed.append((src, dst, ss, rr, dl, y_to))
    order = [(dz, dv, ac) for dz in (2, 1, 3, 0) for dv in (1, 0) for ac in (0, 1)]
    left = []
    for n, (dz, dv, ac) in enumerate(order):
        z_to, v_to, k_to = lax.rem(z + dz, 4), lax.rem(v + dv, 2), lax.rem(k + ac, 2)
        here = lb.at[xh, y, z, xl, k]
        if (dz, dv, ac) == (0, 0, 0):
            pltpu.make_async_copy(fl.at[z_to, v_to, k_to], here, la_r.at[n]).start()
        else:
            copy = remote(
                fl.at[z_to, v_to, k_to], here, la_s.at[n], la_r.at[n], dev(xh, k_to, z_to, y, lax.rem(xl + dv, 2))
            )
            copy.start()
            left.append(copy)

    def l_piece(i, j, part, half):
        if half is None:
            return lb.at[j, i, pl.ds(2 * part, 2)]
        return lb.at[j, i, 2 * part + half]

    def block_piece(buf, depth, core):
        def piece(i, j, part, half):
            if half is None:
                return buf.at[i, j, 2 * core + part]
            return buf.at[i, j, 2 * core + part, pl.ds(half * depth, depth)]

        return piece

    y_up, y_down = dev(xh, k, z, lax.rem(y + 1, 4), xl), dev(xh, k, z, lax.rem(y + 3, 4), xl)
    z_up, z_down = dev(xh, k, lax.rem(z + 1, 4), y, xl), dev(xh, k, lax.rem(z + 3, 4), y, xl)
    u_pair, v_pair = dev(1 - xh, k, z, y, 1 - xl), dev(xh, k, z, y, 1 - xl)
    sib = dev(xh, 1 - k, z, y, xl)
    lg = Gather(l_piece, y, xh, y_up, y_down, u_pair, lg_s, lg_r)
    rg = Gather(block_piece(rb, 4, k), z, xl, z_up, z_down, v_pair, rg_s, rg_r, (sib, rd_s, rd_r))
    tg = Gather(block_piece(tb, 8, k), z, xl, z_up, z_down, v_pair, tg_s, tg_r, (sib, td_s, td_r))

    def own_arrived(dst, ss, rr):
        for n in range(2):
            ref = dst.at[z, xl, 2 * k + n]
            remote(ref, ref, ss.at[n], rr.at[n], sib).wait_recv()

    own_arrived(rb, ra_s, ra_r)
    rg.begin()
    for n, (dz, dv, ac) in enumerate(order):
        ref = lb.at[xh, y, lax.rem(z - dz + 4, 4), lax.rem(xl + dv, 2), lax.rem(k + ac, 2)]
        remote(ref, ref, la_s.at[n], la_r.at[n], sib).wait_recv()
    lg.begin()
    own_arrived(tb, ta_s, ta_r)
    early, late = (9, 0, 1, 12, 13, 10, 11), (4, 5, 6, 2, 3, 14, 15, 7, 8, 16, 17)
    early = (9, 0, 1, 10, 11)
    late = (4, 12, 13, 5, 6, 2, 3, 14, 15, 16, 17, 7, 8)
    for e in early:
        rg.event(e)
        lg.event(e)
    tg.begin()
    for e in late:
        rg.event(e)
        lg.event(e)
    for e in early + late:
        tg.event(e)
    rg.sibling_wait(block_piece(rb, 4, 1 - k))
    tg.sibling_wait(block_piece(tb, 8, 1 - k))

    def gram(step, carry):
        n, h = step // 2, lax.rem(step, 2)
        for kc in range(2):
            total = jnp.zeros((256, 256), F32)
            for yy in range(4):
                lhs = jnp.concatenate([lb[h, yy, zz, x, kc] for zz in range(4) for x in range(2)], axis=1)
                rhs = jnp.concatenate(
                    [
                        jnp.concatenate([rb[zz, x, yy, 2 * n], rb[zz, x, yy, 2 * n + 1]], axis=1)
                        for zz in range(4)
                        for x in range(2)
                    ],
                    axis=0,
                )
                total = total + jnp.dot(lhs, rhs, preferred_element_type=F32)
            low = lax.broadcasted_iota(jnp.int32, (32, 128), 1) < 64
            for aa in range(4):
                for q in range(2):
                    x0 = total[aa * 64 : aa * 64 + 32, q * 128 : q * 128 + 128]
                    x1 = total[aa * 64 + 32 : aa * 64 + 64, q * 128 : q * 128 + 128]
                    y0 = jnp.where(low, x0, pltpu.roll(x1, 64, 1)).astype(BF)
                    y1 = jnp.where(low, pltpu.roll(x0, 64, 1), x1).astype(BF)
                    row = pl.multiple_of((2 * n + q) * 256 + h * 64 + kc * 32, 32)
                    w[pl.ds(row, 32), aa * 128 : aa * 128 + 128] = y0
                    w[pl.ds(row + 128, 32), aa * 128 : aa * 128 + 128] = y1
        return carry

    lax.fori_loop(0, 8, gram, 0)

    def ladder(step, carry):
        quarter, half = step // 2, lax.rem(step, 2)
        for m in range(2):
            lhs = jnp.concatenate(
                [
                    jnp.concatenate([tb[quarter, x, yy, dd] for dd in range(16)], axis=1)
                    for yy in (2 * m, 2 * m + 1)
                    for x in range(2)
                ],
                axis=0,
            )
            col = pl.multiple_of(half * 256, 256)
            got = jnp.dot(lhs, w[:, pl.ds(col, 256)], preferred_element_type=F32)
            pb[quarter, m * 256 : m * 256 + 256, pl.ds(col, 256)] = got.astype(BF)
        return carry

    lax.fori_loop(0, 8, ladder, 0)

    slot = v * 8 + xh * 4 + y
    mine = xl == k
    pieces = []
    for qt in range(4):
        for dy in (2, 1, 3, 0):
            ya = lax.rem(y + dy, 4)
            pi, ka = qt // 2, qt % 2
            src = pb.at[qt, :, pl.ds(pl.multiple_of(ya * 128, 128), 128)]
            n = qt * 4 + dy
            copy = remote(src, rs.at[slot], rs_s.at[n], rs_r.at[slot], dev(pi, ka, z, ya, k))
            if dy == 0:
                own = jnp.logical_and(mine, qt == g)

                @pl.when(own)
                def _():
                    pltpu.make_async_copy(src, rs.at[slot], rs_r.at[slot]).start()

                @pl.when(jnp.logical_not(own))
                def _():
                    copy.start()

                pieces.append((copy, jnp.logical_not(own)))
            else:
                copy.start()
                pieces.append((copy, None))

    for src, dst, ss, rr, dl, y_to in routed:

        @pl.when(y_to != y)
        def _():
            remote(src.at[dl], dst.at[z, xl, y], ss.at[dl], rr.at[ylo], sib).wait_send()

    for copy in left:
        copy.wait_send()
    lg.finish()
    rg.finish()
    tg.finish()

    for n in range(2):
        for m in range(8):
            ref = rs.at[n * 8 + m]
            remote(ref, ref, rs_s.at[0], rs_r.at[n * 8 + m], sib).wait_recv()
        total = rs[n * 8].astype(F32)
        for m in range(1, 8):
            total = total + rs[n * 8 + m].astype(F32)
        out[n * 128 : n * 128 + 128, :] = total.T.astype(BF)
    for copy, when in pieces:
        if when is None:
            copy.wait_send()
        else:

            @pl.when(when)
            def _():
                copy.wait_send()


def on_device(factors, amplitudes, tile_mask):
    g, t = lax.axis_index("grp"), lax.axis_index("tile")
    fl = factors.reshape(128, 32, 4, 4, 2, 2, 2).transpose(2, 5, 4, 3, 6, 1, 0).reshape(4, 2, 2, 256, 128)
    fr = factors[:, :, :NB].reshape(128, 2, 8, 2, NB).transpose(1, 2, 0, 3, 4).reshape(2, 8, 128, 128)
    amp_mask = jnp.repeat(tile_mask[t, :, g // 2], 64).astype(BF)
    screened = amplitudes * amp_mask[None, None, :]
    tt = screened.reshape(64, 2, 16, 128).transpose(1, 2, 0, 3)
    dma = pltpu.SemaphoreType.DMA
    any_space = pl.BlockSpec(memory_space=pl.ANY)
    result = pl.pallas_call(
        kernel,
        name="ladder",
        out_shape=jax.ShapeDtypeStruct((256, 512), BF),
        in_specs=[any_space] * 3,
        out_specs=pl.BlockSpec(memory_space=pltpu.VMEM),
        scratch_shapes=[
            pltpu.VMEM((2, 4, 4, 2, 2, 256, 128), BF),
            pltpu.VMEM((4, 2, 4, 8, 128, 128), BF),
            pltpu.VMEM((4, 2, 4, 16, 64, 128), BF),
            pltpu.VMEM((8, 128), F32),
            pltpu.VMEM((2048, 512), BF),
            pltpu.VMEM((4, 512, 512), BF),
            pltpu.VMEM((16, 512, 128), BF),
            dma((16,)), dma((16,)), dma((2,)), dma((2,)), dma((2,)), dma((2,)),
            dma((18,)), dma((18,)), dma((18,)), dma((18,)), dma((18,)), dma((18,)),
            dma((20,)), dma((20,)), dma((20,)), dma((20,)), dma((16,)), dma((16,)),
        ],
        compiler_params=pltpu.CompilerParams(has_side_effects=True, vmem_limit_bytes=60 * 1024 * 1024),
    )(fl, fr, tt)
    res_mask = jnp.repeat(lax.dynamic_slice(tile_mask[:, t // 16, 0], (g * 8,), (8,)), 64).astype(BF)
    return result.reshape(4, NB, 512) * res_mask[None, None, :]


def solution(mesh):
    placed = (P("tile", "grp", None), P("tile", "grp", None), P())
    return jax.shard_map(
        on_device, mesh=mesh, in_specs=placed, out_specs=P("tile", None, "grp"), check_vma=False
    )
```

time: 862 us -> 164 us (0.19)
  waiting for transfers between devices: 728 us -> 0 us
  Pallas kernels: 0 us -> 154 us
  local copies, waits for them, and re-layouts: 63.3 us -> 6.78 us
  blocking collectives: 26.4 us -> 0 us
  matrix products: 23.4 us -> 0 us
  between operations: 13.3 us -> 0.05 us
    all_gather x3 -> x0, waiting for transfers between devices: 716 us -> none  [the longest x1 345 us: on_device(): window_all = lax.all_gather(window, 'tile', axis=0, tiled=True)]
    pallas_call x0 -> x1, Pallas kernels: none -> 154 us  [on_device(): pl.pallas_call(kernel, name='ladder', out_shape=jax.ShapeDtypeStruct((256...]
    all_gather x2 -> x0, local copies, waits for them, and re-layouts: 30 us -> none  [the longest x1 22.6 us: on_device(): piece = lax.all_gather(screened, 'tile', axis=0, tiled=True)]
    all_to_all x1 -> x0, blocking collectives: 26.4 us -> none  [on_device(): lax.all_to_all(factors, 'tile', split_axis=2, concat_axis=0, tiled=True)]
    dot_general x2 -> x0, matrix products: 23.4 us -> none  [the longest x1 13.6 us: on_device(): lax.dot_general(left_matrix, window_matrix, (((0,), (0,)), ((), ())), pre...]
    reshape x3 -> x1, local copies, waits for them, and re-layouts: 13.4 us -> 1.04 us  [on_device(): factors[:, :, :NB].reshape(128, 2, 8, 2, NB).transpose(1, 2, 0, 3, 4)]
    all_to_all x1 -> x0, waiting for transfers between devices: 11.1 us -> none  [sent_and_summed(): tiles = lax.all_to_all(in_blocks(value, dim, peers), axis, 0, 0, tiled=True)]
  transfers between devices with their start and end apart: 4 -> 0, of which waited for: 4 -> 0; matrix products, arithmetic and copies ran while one was open for 6% -> 0% of each run, Pallas kernels for 0% -> 0%
where the time goes in v1:
time: 164 us
  Pallas kernels  154 us (94%)
  local copies, waits for them, and re-layouts  6.78 us (4%)
  other arithmetic  3.09 us (2%)
    pallas_call x1, Pallas kernels, on_device(): pl.pallas_call(kernel, name='ladder', out_shape=jax.ShapeDtypeStruct((256...  154 us

profile of v1, /device:TPU:1, one launch (start us, length us, event | category | flops | bytes accessed | tf_op | source)
XLA Modules:
  0.0 163.6 jit_solution(17380504829073581857)
XLA Ops:
  0.0 0.0 copy-start.1
  0.0 0.7 copy-done.1
  0.7 0.2 convert_reduce_fusion
  0.9 0.1 broadcast_in_dim.8
  0.9 0.1 convert_element_type.30
  1.0 0.0 copy-start
  1.0 1.2 broadcast_multiply_fusion
  2.2 1.0 copy.10
  3.2 0.0 copy-done
  3.2 1.5 copy.7
  4.7 1.1 copy.8
  5.8 1.1 copy.9
  6.9 1.0 copy.11.fr
  8.0 153.7 %ladder.1 = bf16[256,512]{1,0:T(8,128)(2,1)} custom-call(bf16[4,2,2,256,128]{4,3,2,1,0:T(8,128)(2,1)} %bitcast.17, bf16[2,8,128,128]{3,2,1,0:T(8,128)(2,1)} %copy.11.fr, bf16[2,16,64,128]{3,2,1,0:T(8,128)(2,1)} %bitcast.20), custom_call_target="tpu_custom_call" | custom-call | tf_op jit(solution)/shard_map/ladder/pallas_call | solution.py:292
  161.7 0.1 convert_bitcast_fusion
  161.8 0.1 broadcast_in_dim.9
  161.8 0.1 convert_element_type.33
  161.9 1.7 %broadcast_multiply_fusion.1 = bf16[4,64,512]{2,1,0:T(8,128)(2,1)} fusion(bf16[4,64,512]{2,1,0:T(8,128)(2,1)} %bitcast.21, bf16[512]{0:T(512)(128)(2,1)S(1)} %convert_element_type.33), kind=kLoop, calls=%fused_computation.1 | loop fusion | flops 131072 | bytes 525312 | tf_op jit(solution)/shard_map/mul | solution.py:313
Async XLA Ops:
  0.0 0.7 copy-start.1
  1.0 2.2 %copy-start = (bf16[128,32,128]{2,1,0:T(8,128)(2,1)S(1)}, bf16[128,32,128]{2,1,0:T(8,128)(2,1)}, u32[]{:S(2)}) copy-start(bf16[128,32,128]{2,1,0:T(8,128)(2,1)} %param.3) | copy-start | bytes 3145732

commit v2 on v1

v2 whole, which is shorter than its diff:
```python
import functools

import jax
import jax.numpy as jnp
from jax import lax
from jax.experimental import pallas as pl
from jax.experimental.pallas import tpu as pltpu
from jax.sharding import PartitionSpec as P

MESH = pl.DeviceIdType.MESH
NB = 64
BF = jnp.bfloat16
F32 = jnp.float32
SUBS = [(dz, dv, ac) for dz, dv in ((0, 0), (1, 0), (3, 0), (0, 1), (1, 1), (3, 1), (2, 0), (2, 1)) for ac in (0, 1)]
SPANS = {(0, None): (0, 7), (0, 0): (0, 4), (0, 1): (4, 3), (1, None): (7, 9), (1, 0): (7, 4), (1, 1): (11, 5)}
PLAN = (
    "l4", "l0", "l1", "r4", "r0", "r1", "r9", "r10", "r11", "r3", "r2", "r5",
    "r13", "r12", "l9", "l10", "l11", "r6", "TB", "r14", "r15", "r8", "l3", "l2",
    "r7", "r16", "r17", "RS", "G00", "l5", "t0", "t1", "G10", "t4", "G03", "t10",
    "t11", "l13", "l12", "t2", "t3", "t9", "l6", "G01", "t5", "G13", "l14", "l15",
    "l8", "t14", "t15", "t12", "t13", "G11", "t6", "t7", "G02", "l7", "l16", "t8",
    "l17", "t16", "t17", "G12", "TS",
)


def remote(src, dst, send, recv, dev):
    return pltpu.make_async_remote_copy(
        src_ref=src, dst_ref=dst, send_sem=send, recv_sem=recv, device_id=dev, device_id_type=MESH
    )


class Gather:
    def __init__(self, name, piece, i, j, up, down, pair, send, recv, sibling=None):
        self.name, self.piece, self.i, self.j = name, piece, i, j
        self.pair = pair
        self.send, self.recv = send, recv
        self.sibling = sibling
        self.sent = []
        i1, i2, i3, o = lax.rem(i + 1, 4), lax.rem(i + 2, 4), lax.rem(i + 3, 4), 1 - j
        self.brings = [
            (i3, j, 0, None), (i1, j, 0, None), (i2, j, 0, 0), (i2, j, 0, 1),
            (i, o, 0, None), (i3, o, 0, None), (i1, o, 0, None), (i2, o, 0, 0), (i2, o, 0, 1),
            (i, o, 1, None),
            (i3, j, 1, None), (i1, j, 1, None), (i3, o, 1, None), (i1, o, 1, None),
            (i2, j, 1, 0), (i2, j, 1, 1), (i2, o, 1, 0), (i2, o, 1, 1),
        ]
        self.sends = [
            ((i, j, 0, None), up), ((i, j, 0, None), down), ((i3, j, 0, 0), up), ((i1, j, 0, 1), down),
            ((i, j, 0, None), pair), ((i3, j, 0, None), pair), ((i1, j, 0, None), pair), ((i2, j, 0, 0), pair), ((i2, j, 0, 1), pair),
            ((i, j, 1, None), pair),
            ((i, j, 1, None), up), ((i, j, 1, None), down), ((i, o, 1, None), up), ((i, o, 1, None), down),
            ((i3, j, 1, 0), up), ((i1, j, 1, 1), down), ((i3, o, 1, 0), up), ((i1, o, 1, 1), down),
        ]
        self.then = {0: (2, 5), 1: (3, 6), 2: (7,), 3: (8,), 9: (12, 13), 10: (14,), 11: (15,), 12: (16,), 13: (17,)}

    def _go(self, e):
        where, dev = self.sends[e]
        ref = self.piece(*where)
        copy = remote(ref, ref, self.send.at[e], self.recv.at[e], dev)
        copy.start()
        self.sent.append(copy)

    def _share(self, slot, where):
        if self.sibling is not None:
            dev, send, recv = self.sibling
            ref = self.piece(*where)
            copy = remote(ref, ref, send.at[slot], recv.at[slot], dev)
            copy.start()
            self.sent.append(copy)

    def begin(self, part):
        for e in ((0, 1, 4), (9, 10, 11))[part]:
            self._go(e)
        self._share(18 + part, (self.i, self.j, part, None))

    def event(self, e):
        with jax.named_scope(self.name + str(e)):
            ref = self.piece(*self.brings[e])
            remote(ref, ref, self.send.at[e], self.recv.at[e], self.pair).wait_recv()
            for s in self.then.get(e, ()):
                self._go(s)
            self._share(e, self.brings[e])

    def sibling_wait(self, other_piece):
        dev, send, recv = self.sibling
        with jax.named_scope(self.name + "_sib"):
            for slot in range(20):
                where = self.brings[slot] if slot < 18 else (self.i, self.j, slot - 18, None)
                ref = other_piece(*where)
                remote(ref, ref, send.at[slot], recv.at[slot], dev).wait_recv()

    def finish(self):
        for copy in self.sent:
            copy.wait_send()


def kernel(
    mask, fl, fr, tt, out,
    lb, rb, tb, gr, w, pb, rs,
    la_s, la_r, ra_s, ra_r, ta_s, ta_r,
    lg_s, lg_r, rg_s, rg_r, tg_s, tg_r,
    rd_s, rd_r, td_s, td_r, rs_s, rs_r,
):
    g, t = lax.axis_index("grp"), lax.axis_index("tile")
    xh, k = g // 2, lax.rem(g, 2)
    z, y, xl = t // 8, lax.rem(t // 2, 4), lax.rem(t, 2)
    v = lax.rem(xl + xh, 2)

    def dev(xh_, k_, z_, y_, xl_):
        return {"grp": xh_ * 2 + k_, "tile": z_ * 8 + y_ * 2 + xl_}

    barrier = pltpu.get_barrier_semaphore()
    with jax.named_scope("barrier"):
        count = 0
        for dz in range(4):
            for dy in range(4):
                for dh in range(2):
                    for dl in range(2):
                        for dk in range(2):
                            same_z = dz == 0
                            same_yh = dy == 0 and dh == 0
                            if (dz, dy, dh, dl, dk) == (0, 0, 0, 0, 0) or not (same_z or same_yh):
                                continue
                            pl.semaphore_signal(
                                barrier, inc=1,
                                device_id=dev(lax.rem(xh + dh, 2), lax.rem(k + dk, 2), lax.rem(z + dz, 4), lax.rem(y + dy, 4), lax.rem(xl + dl, 2)),
                                device_id_type=MESH,
                            )
                            count += 1
        pl.semaphore_wait(barrier, count)

    yhi, ylo = y // 2, lax.rem(y, 2)
    routed = []

    def route(src, dst, ss, rr, depth):
        for dl in range(2):
            y_to = 2 * k + dl
            here = dst.at[z, xl, pl.ds(y * depth, depth)]

            @pl.when(y_to == y)
            def _():
                pltpu.make_async_copy(src.at[dl], here, rr.at[ylo]).start()

            @pl.when(y_to != y)
            def _():
                remote(src.at[dl], here, ss.at[dl], rr.at[ylo], dev(xh, yhi, z, y_to, xl)).start()

            routed.append((src.at[dl], here, ss.at[dl], rr.at[ylo], y_to))

    left = []
    with jax.named_scope("issue"):
        for n, (dz, dv, ac) in enumerate(SUBS):
            z_to, v_to, k_to = lax.rem(z + dz, 4), lax.rem(v + dv, 2), lax.rem(k + ac, 2)
            src, here = fl.at[z_to, :, k_to, v_to], lb.at[xh, y, n]
            if n == 0:
                pltpu.make_async_copy(src, here, la_r.at[n]).start()
            else:
                copy = remote(src, here, la_s.at[n], la_r.at[n], dev(xh, k_to, z_to, y, lax.rem(xl + dv, 2)))
                copy.start()
                left.append(copy)
            if n == 3:
                route(fr, rb, ra_s, ra_r, 8)

    def l_piece(i, j, part, half):
        first, some = SPANS[part, half]
        return lb.at[j, i, pl.ds(first, some)]

    def block_piece(buf, scale, core):
        def piece(i, j, part, half):
            first, some = SPANS[part, half]
            return buf.at[i, j, pl.ds((core * 16 + first) * scale, some * scale)]

        return piece

    y_up, y_down = dev(xh, k, z, lax.rem(y + 1, 4), xl), dev(xh, k, z, lax.rem(y + 3, 4), xl)
    z_up, z_down = dev(xh, k, lax.rem(z + 1, 4), y, xl), dev(xh, k, lax.rem(z + 3, 4), y, xl)
    u_pair, v_pair = dev(1 - xh, k, z, y, 1 - xl), dev(xh, k, z, y, 1 - xl)
    sib = dev(xh, 1 - k, z, y, xl)
    lg = Gather("l", l_piece, y, xh, y_up, y_down, u_pair, lg_s, lg_r)
    rg = Gather("r", block_piece(rb, 1, k), z, xl, z_up, z_down, v_pair, rg_s, rg_r, (sib, rd_s, rd_r))
    tg = Gather("t", block_piece(tb, 2, k), z, xl, z_up, z_down, v_pair, tg_s, tg_r, (sib, td_s, td_r))

    def own_arrived(dst, ss, rr, depth, n):
        ref = dst.at[z, xl, pl.ds((2 * k + n) * depth, depth)]
        remote(ref, ref, ss.at[n], rr.at[n], sib).wait_recv()

    def left_arrived(n):
        ref = lb.at[xh, y, n]
        remote(ref, ref, la_s.at[n], la_r.at[n], sib).wait_recv()

    def gram(h_rel, dy, place):
        h, yy = lax.rem(xh + h_rel, 2), lax.rem(y + dy, 4)

        def step(n, carry):
            rhs = []
            for dz, dv, ac in SUBS[::2]:
                zz, x = lax.rem(z - dz + 4, 4), lax.rem(xl + xh + dv + h, 2)
                rhs.append(jnp.concatenate([rb[zz, x, yy * 8 + 2 * n], rb[zz, x, yy * 8 + 2 * n + 1]], axis=1))
            rhs = jnp.concatenate(rhs, axis=0)
            col = pl.ds(pl.multiple_of(n * 256, 256), 256)
            low = lax.broadcasted_iota(jnp.int32, (32, 128), 1) < 64
            for ac in range(2):
                lhs = jnp.concatenate([lb[h, yy, 2 * s + ac].reshape(256, 128) for s in range(8)], axis=1)
                got = jnp.dot(lhs, rhs, preferred_element_type=F32)
                if place != "first":
                    got = got + gr[h_rel, ac, :, col]
                if place != "last":
                    gr[h_rel, ac, :, col] = got
                    continue
                row = h * 64 + lax.rem(k + ac, 2) * 32
                for aa in range(4):
                    for q in range(2):
                        x0 = got[aa * 64 : aa * 64 + 32, q * 128 : q * 128 + 128]
                        x1 = got[aa * 64 + 32 : aa * 64 + 64, q * 128 : q * 128 + 128]
                        y0 = jnp.where(low, x0, pltpu.roll(x1, 64, 1)).astype(BF)
                        y1 = jnp.where(low, pltpu.roll(x0, 64, 1), x1).astype(BF)
                        at0 = pl.multiple_of((2 * n + q) * 256 + row, 32)
                        w[pl.ds(at0, 32), aa * 128 : aa * 128 + 128] = y0
                        w[pl.ds(at0 + 128, 32), aa * 128 : aa * 128 + 128] = y1
            return carry

        lax.fori_loop(0, 4, step, 0)

    with jax.named_scope("own_r"):
        own_arrived(rb, ra_s, ra_r, 8, 0)
        rg.begin(0)
        own_arrived(rb, ra_s, ra_r, 8, 1)
        rg.begin(1)
        route(tt, tb, ta_s, ta_r, 16)
    with jax.named_scope("own_l"):
        for n in range(7):
            left_arrived(n)
        lg.begin(0)
    with jax.named_scope("own_lb"):
        for n in range(7, 16):
            left_arrived(n)
        lg.begin(1)
    gathers = {"l": lg, "r": rg, "t": tg}
    for word in PLAN:
        if word == "TB":
            with jax.named_scope("own_t"):
                own_arrived(tb, ta_s, ta_r, 16, 0)
                tg.begin(0)
                own_arrived(tb, ta_s, ta_r, 16, 1)
                tg.begin(1)
        elif word == "RS":
            rg.sibling_wait(block_piece(rb, 1, 1 - k))
        elif word == "TS":
            tg.sibling_wait(block_piece(tb, 2, 1 - k))
        elif word[0] == "G":
            place = "last" if word[2] == "2" else "first" if word[2] == "0" else "more"
            with jax.named_scope(word):
                gram(int(word[1]), int(word[2]), place)
        else:
            gathers[word[0]].event(int(word[1:]))

    slot = v * 8 + xh * 4 + y
    mine = xl == k

    def piece(s, dy):
        qt = lax.rem(g + 1 + s, 4)
        ya = lax.rem(y + dy, 4)
        src = pb.at[qt, :, pl.ds(pl.multiple_of(ya * 128, 128), 128)]
        copy = remote(src, rs.at[slot], rs_s.at[s * 4 + dy], rs_r.at[slot], dev(qt // 2, lax.rem(qt, 2), z, ya, k))
        return src, copy

    def ladder(s, carry):
        qt = lax.rem(g + 1 + s, 4)
        low = lax.broadcasted_iota(jnp.int32, (1, 128), 1) < 64
        for m in range(2):
            lhs = []
            for yy in (2 * m, 2 * m + 1):
                for x in range(2):
                    block = (qt * 8 + yy * 2 + x) * 4 + xh
                    keep = jnp.where(low, mask[block], mask[block + 2]).astype(F32).astype(BF)
                    lhs.append(jnp.concatenate([tb[qt, x, yy * 16 + dd] * keep for dd in range(16)], axis=1))
            lhs = jnp.concatenate(lhs, axis=0)
            for half in range(2):
                got = jnp.dot(lhs, w[:, half * 256 : half * 256 + 256], preferred_element_type=F32)
                pb[qt, m * 256 : m * 256 + 256, half * 256 : half * 256 + 256] = got.astype(BF)
        for dy in (2, 1, 3, 0):
            src, copy = piece(s, dy)
            if dy == 0:
                own = jnp.logical_and(mine, s == 3)

                @pl.when(own)
                def _():
                    pltpu.make_async_copy(src, rs.at[slot], rs_r.at[slot]).start()

                @pl.when(jnp.logical_not(own))
                def _():
                    copy.start()

            else:
                copy.start()
        return carry

    with jax.named_scope("ladd"):
        lax.fori_loop(0, 4, ladder, 0)

    with jax.named_scope("drain"):
        for src, here, ss, rr, y_to in routed:

            @pl.when(y_to != y)
            def _():
                remote(src, here, ss, rr, sib).wait_send()

        for copy in left:
            copy.wait_send()
        lg.finish()
        rg.finish()
        tg.finish()

    for n in range(2):
        with jax.named_scope("rs%d" % n):
            for m in range(8):
                ref = rs.at[n * 8 + m]
                remote(ref, ref, rs_s.at[0], rs_r.at[n * 8 + m], sib).wait_recv()
        total = rs[n * 8].astype(F32)
        for m in range(1, 8):
            total = total + rs[n * 8 + m].astype(F32)
        total = total.T
        for m in range(8):
            keep = mask[(g * 8 + m) * 4 + (z // 2) * 2].astype(F32)
            out[n * 128 : n * 128 + 128, m * 64 : m * 64 + 64] = (total[:, m * 64 : m * 64 + 64] * keep).astype(BF)
    with jax.named_scope("drain2"):
        for s in range(4):
            for dy in range(4):
                _, copy = piece(s, dy)
                if (s, dy) == (3, 0):

                    @pl.when(jnp.logical_not(mine))
                    def _():
                        copy.wait_send()

                else:
                    copy.wait_send()


def on_device(factors, amplitudes, tile_mask):
    fl = factors.transpose(2, 1, 0).reshape(4, 4, 2, 2, 2, 32, 128)
    fr = factors[:, :, :NB].reshape(128, 2, 8, 2, NB).transpose(1, 2, 0, 3, 4).reshape(2, 8, 128, 128)
    tt = amplitudes.transpose(1, 0, 2).reshape(2, 16, 64, 128)
    dma = pltpu.SemaphoreType.DMA
    any_space = pl.BlockSpec(memory_space=pl.ANY)
    result = pl.pallas_call(
        kernel,
        name="ladder",
        out_shape=jax.ShapeDtypeStruct((256, 512), BF),
        in_specs=[pl.BlockSpec(memory_space=pltpu.SMEM)] + [any_space] * 3,
        out_specs=pl.BlockSpec(memory_space=pltpu.VMEM),
        scratch_shapes=[
            pltpu.VMEM((2, 4, 16, 4, 2, 32, 128), BF),
            pltpu.VMEM((4, 2, 32, 128, 128), BF),
            pltpu.VMEM((4, 2, 64, 64, 128), BF),
            pltpu.VMEM((2, 2, 256, 1024), F32),
            pltpu.VMEM((2048, 512), BF),
            pltpu.VMEM((4, 512, 512), BF),
            pltpu.VMEM((16, 512, 128), BF),
            dma((16,)), dma((16,)), dma((2,)), dma((2,)), dma((2,)), dma((2,)),
            dma((18,)), dma((18,)), dma((18,)), dma((18,)), dma((18,)), dma((18,)),
            dma((20,)), dma((20,)), dma((20,)), dma((20,)), dma((16,)), dma((16,)),
        ],
        compiler_params=pltpu.CompilerParams(
            collective_id=0, has_side_effects=True, vmem_limit_bytes=60 * 1024 * 1024
        ),
    )(tile_mask.reshape(128), fl, fr, tt)
    return result.reshape(4, NB, 512)


def solution(mesh):
    placed = (P("tile", "grp", None), P("tile", "grp", None), P())
    return jax.shard_map(
        on_device, mesh=mesh, in_specs=placed, out_specs=P("tile", None, "grp"), check_vma=False
    )
```

time: 164 us -> 130 us (0.79)
  the two profiles are of different devices: /device:TPU:1 before, /device:TPU:17 now
where the time goes in v2:
time: 130 us
  Pallas kernels  120 us (92%)
  local copies, waits for them, and re-layouts  9.69 us (7%)
    pallas_call x1, Pallas kernels, on_device(): pl.pallas_call(kernel, name='ladder', out_shape=jax.ShapeDtypeStruct((256...  120 us

profile of v2, /device:TPU:17, one launch (start us, length us, event | category | flops | bytes accessed | tf_op | source)
XLA Modules:
  0.0 129.7 jit_solution(2428854104149696590)
XLA Ops:
  0.0 0.0 copy-start
  0.0 0.9 copy.8
  0.9 0.7 reshape.18.mask
  1.5 2.1 %copy.11 = bf16[32,64,128]{2,1,0:T(8,128)(2,1)} copy(bf16[32,64,128]{2,0,1:T(8,128)(2,1)} %bitcast.17) | data formatting | bytes 1048576 | tf_op jit(solution)/shard_map/transpose | solution.py:343
  3.6 0.0 copy-done
  3.6 1.1 copy.10
  4.7 1.0 copy.12.fr
  5.7 2.3 %copy.9 = bf16[128,32,128]{2,1,0:T(8,128)(2,1)} copy(bf16[128,32,128]{0,1,2:T(8,128)(2,1)S(1)} %bitcast.13) | data formatting | bytes 2097152 | tf_op jit(solution)/shard_map/transpose | solution.py:341
  8.0 120.0 %ladder.1 = bf16[256,512]{1,0:T(8,128)(2,1)} custom-call(s32[128]{0:T(128)} %reshape.18.mask, bf16[4,4,2,2,2,32,128]{6,5,4,3,2,1,0:T(8,128)(2,1)} %bitcast.11, bf16[2,8,128,128]{3,2,1,0:T(8,128)(2,1)} %copy.12.fr, bf16[2,16,64,128]{3,2,1,0:T(8,128)(2,1)} %bitcast.14), custom_call_target="tpu_custom_call" | custom-call | tf_op jit(solution)/shard_map/ladder/pallas_call | solution.py:346
  128.0 1.7 %copy.14 = bf16[4,64,512]{2,1,0:T(8,128)(2,1)} copy(bf16[4,64,512]{2,1,0:T(8,128)(2,1)} %bitcast.16) | data formatting | bytes 524288
Async XLA Ops:
  0.0 3.6 %copy-start = (bf16[128,32,128]{2,1,0:T(8,128)(2,1)S(1)}, bf16[128,32,128]{2,1,0:T(8,128)(2,1)}, u32[]{:S(2)}) copy-start(bf16[128,32,128]{2,1,0:T(8,128)(2,1)} %param.3) | copy-start | bytes 3145732

commit v3 on v2

--- a/solution.py
+++ b/solution.py
@@ -13,9 +13,11 @@
 F32 = jnp.float32
 SUBS = [(dz, dv, ac) for dz, dv in ((0, 0), (1, 0), (3, 0), (0, 1), (1, 1), (3, 1), (2, 0), (2, 1)) for ac in (0, 1)]
 SPANS = {(0, None): (0, 7), (0, 0): (0, 4), (0, 1): (4, 3), (1, None): (7, 9), (1, 0): (7, 4), (1, 1): (11, 5)}
+BLOCK_SPANS = {(0, None): (0, 7), (0, 0): (0, 2), (0, 1): (2, 5), (1, None): (7, 9), (1, 0): (7, 3), (1, 1): (10, 6)}
+STEP = {0: 0, 1: 1, 3: 2}
 PLAN = (
     "l4", "l0", "l1", "r4", "r0", "r1", "r9", "r10", "r11", "r3", "r2", "r5",
-    "r13", "r12", "l9", "l10", "l11", "r6", "TB", "r14", "r15", "r8", "l3", "l2",
+    "r13", "r12", "TB", "l9", "l10", "l11", "r6", "r14", "r15", "r8", "l3", "l2",
     "r7", "r16", "r17", "RS", "G00", "l5", "t0", "t1", "G10", "t4", "G03", "t10",
     "t11", "l13", "l12", "t2", "t3", "t9", "l6", "G01", "t5", "G13", "l14", "l15",
     "l8", "t14", "t15", "t12", "t13", "G11", "t6", "t7", "G02", "l7", "l16", "t8",
@@ -96,10 +98,10 @@
 
 def kernel(
     mask, fl, fr, tt, out,
-    lb, rb, tb, gr, w, pb, rs,
+    lb, rb, tb, gr, w, pb, m1, m2, rs,
     la_s, la_r, ra_s, ra_r, ta_s, ta_r,
     lg_s, lg_r, rg_s, rg_r, tg_s, tg_r,
-    rd_s, rd_r, td_s, td_r, rs_s, rs_r,
+    rd_s, rd_r, td_s, td_r, m1_s, m1_r, far_s, m2_r, near_s, rs_r,
 ):
     g, t = lax.axis_index("grp"), lax.axis_index("tile")
     xh, k = g // 2, lax.rem(g, 2)
@@ -167,7 +169,7 @@
 
     def block_piece(buf, scale, core):
         def piece(i, j, part, half):
-            first, some = SPANS[part, half]
+            first, some = BLOCK_SPANS[part, half]
             return buf.at[i, j, pl.ds((core * 16 + first) * scale, some * scale)]
 
         return piece
@@ -254,49 +256,128 @@
         else:
             gathers[word[0]].event(int(word[1:]))
 
-    slot = v * 8 + xh * 4 + y
-    mine = xl == k
-
-    def piece(s, dy):
-        qt = lax.rem(g + 1 + s, 4)
-        ya = lax.rem(y + dy, 4)
-        src = pb.at[qt, :, pl.ds(pl.multiple_of(ya * 128, 128), 128)]
-        copy = remote(src, rs.at[slot], rs_s.at[s * 4 + dy], rs_r.at[slot], dev(qt // 2, lax.rem(qt, 2), z, ya, k))
-        return src, copy
-
-    def ladder(s, carry):
-        qt = lax.rem(g + 1 + s, 4)
+    home = xl == k
+    away = jnp.logical_not(home)
+
+    def p_piece(pi, ka, e):
+        ya = lax.rem(y + e, 4)
+        return pb.at[2 * pi + ka, :, pl.ds(pl.multiple_of(ya * 128, 128), 128)]
+
+    def cross(pi, ka):
+        return remote(p_piece(pi, ka, 2), m1.at[ka, pi], m1_s.at[ka, pi], m1_r.at[ka, pi], (y_up, y_down)[ka])
+
+    def to_pair(ka, e):
+        n = ka * 3 + STEP[e]
+        return remote(p_piece(1 - xh, ka, e), m2.at[n], far_s.at[n], m2_r.at[n], u_pair)
+
+    def to_far(ka, e):
+        n = ka * 3 + STEP[e]
+        slot = 6 + STEP[e]
+        owner = dev(1 - xh, ka, z, lax.rem(y + e, 4), 1 - xl)
+        return remote(p_piece(1 - xh, ka, e), rs.at[slot], far_s.at[n], rs_r.at[slot], owner)
+
+    def to_near(ka, e, kind):
+        n = ka * 3 + STEP[e]
+        slot = 3 * kind + STEP[e]
+        owner = dev(xh, ka, z, lax.rem(y + e, 4), (xl, 1 - xl)[kind])
+        return remote(p_piece(xh, ka, e), rs.at[slot], near_s.at[n], rs_r.at[slot], owner)
+
+    def send_far(ka, e):
+        @pl.when(home)
+        def _():
+            to_pair(ka, e).start()
+
+        @pl.when(away)
+        def _():
+            to_far(ka, e).start()
+
+    def send_home(ka, e):
+        if e != 0:
+            to_near(ka, e, 0).start()
+            return
+
+        @pl.when(k == ka)
+        def _():
+            pltpu.make_async_copy(p_piece(xh, ka, 0), rs.at[0], rs_r.at[0]).start()
+
+        @pl.when(k != ka)
+        def _():
+            to_near(ka, 0, 0).start()
+
+    def ladder(qt):
         low = lax.broadcasted_iota(jnp.int32, (1, 128), 1) < 64
-        for m in range(2):
+
+        def rows(m, carry):
             lhs = []
-            for yy in (2 * m, 2 * m + 1):
+            for yy in range(2):
                 for x in range(2):
-                    block = (qt * 8 + yy * 2 + x) * 4 + xh
-                    keep = jnp.where(low, mask[block], mask[block + 2]).astype(F32).astype(BF)
-                    lhs.append(jnp.concatenate([tb[qt, x, yy * 16 + dd] * keep for dd in range(16)], axis=1))
+                    yyy = 2 * m + yy
+                    block = qt * 8 + yyy * 2 + x
+                    keep = jnp.where(low, mask[0, xh, block], mask[1, xh, block]).astype(F32).astype(BF)
+                    lhs.append(jnp.concatenate([tb[qt, x, yyy * 16 + dd] * keep for dd in range(16)], axis=1))
             lhs = jnp.concatenate(lhs, axis=0)
+            at = pl.ds(pl.multiple_of(m * 256, 256), 256)
             for half in range(2):
                 got = jnp.dot(lhs, w[:, half * 256 : half * 256 + 256], preferred_element_type=F32)
-                pb[qt, m * 256 : m * 256 + 256, half * 256 : half * 256 + 256] = got.astype(BF)
-        for dy in (2, 1, 3, 0):
-            src, copy = piece(s, dy)
-            if dy == 0:
-                own = jnp.logical_and(mine, s == 3)
-
-                @pl.when(own)
-                def _():
-                    pltpu.make_async_copy(src, rs.at[slot], rs_r.at[slot]).start()
-
-                @pl.when(jnp.logical_not(own))
-                def _():
-                    copy.start()
-
-            else:
-                copy.start()
-        return carry
+                pb[qt, at, half * 256 : half * 256 + 256] = got.astype(BF)
+            return carry
+
+        lax.fori_loop(0, 2, rows, 0)
+
+    def merge(pi, ka, e, other):
+        ya = lax.rem(y + e, 4)
+        at = pl.ds(pl.multiple_of(ya * 128, 128), 128)
+        pb[2 * pi + ka, :, at] = (pb[2 * pi + ka, :, at].astype(F32) + other[...].astype(F32)).astype(BF)
 
     with jax.named_scope("ladd"):
-        lax.fori_loop(0, 4, ladder, 0)
+        for pi, ka in ((1 - xh, 0), (1 - xh, 1), (xh, 0), (xh, 1)):
+            ladder(2 * pi + ka)
+            cross(pi, ka).start()
+            for e in (0, (3, 1)[ka]):
+                if pi is xh:
+
+                    @pl.when(home)
+                    def _():
+                        send_home(ka, e)
+
+                else:
+                    send_far(ka, e)
+
+    def take_cross(pi, ka):
+        e = (1, 3)[ka]
+        ref = m1.at[ka, pi]
+        remote(ref, ref, m1_s.at[ka, pi], m1_r.at[ka, pi], sib).wait_recv()
+        merge(pi, ka, e, ref)
+        return e
+
+    def take_pair(ka, e):
+        n = ka * 3 + STEP[e]
+        ref = m2.at[n]
+        remote(ref, ref, far_s.at[n], m2_r.at[n], sib).wait_recv()
+        merge(xh, ka, e, ref)
+        to_near(ka, e, 1).start()
+
+    with jax.named_scope("merge"):
+
+        @pl.when(home)
+        def _():
+            for ka in range(2):
+                to_pair(ka, take_cross(1 - xh, ka)).start()
+            for ka in range(2):
+                send_home(ka, take_cross(xh, ka))
+
+        @pl.when(away)
+        def _():
+            take_pair(0, 0)
+            take_pair(0, 3)
+            for ka in range(2):
+                to_far(ka, take_cross(1 - xh, ka)).start()
+            take_pair(1, 0)
+            take_pair(1, 1)
+            for ka in range(2):
+                take_cross(xh, ka)
+            take_pair(0, 1)
+            take_pair(1, 3)
 
     with jax.named_scope("drain"):
         for src, here, ss, rr, y_to in routed:
@@ -311,30 +392,45 @@
         rg.finish()
         tg.finish()
 
-    for n in range(2):
-        with jax.named_scope("rs%d" % n):
-            for m in range(8):
-                ref = rs.at[n * 8 + m]
-                remote(ref, ref, rs_s.at[0], rs_r.at[n * 8 + m], sib).wait_recv()
-        total = rs[n * 8].astype(F32)
-        for m in range(1, 8):
-            total = total + rs[n * 8 + m].astype(F32)
-        total = total.T
+    def gathered(slots):
+        total = None
+        for n in slots:
+            ref = rs.at[n]
+            with jax.named_scope("rs%d" % n):
+                remote(ref, ref, near_s.at[0], rs_r.at[n], sib).wait_recv()
+            part = rs[n].astype(F32)
+            total = part if total is None else total + part
+        return total.T
+
+    for half, slots in ((v, (0, 6, 1, 2, 7, 8)), (1 - v, (3, 4, 5))):
+        total = gathered(slots)
+        at = pl.ds(pl.multiple_of(half * 128, 128), 128)
         for m in range(8):
-            keep = mask[(g * 8 + m) * 4 + (z // 2) * 2].astype(F32)
-            out[n * 128 : n * 128 + 128, m * 64 : m * 64 + 64] = (total[:, m * 64 : m * 64 + 64] * keep).astype(BF)
+            keep = mask[z // 2, 0, g * 8 + m].astype(F32)
+            out[at, m * 64 : m * 64 + 64] = (total[:, m * 64 : m * 64 + 64] * keep).astype(BF)
     with jax.named_scope("drain2"):
-        for s in range(4):
-            for dy in range(4):
-                _, copy = piece(s, dy)
-                if (s, dy) == (3, 0):
-
-                    @pl.when(jnp.logical_not(mine))
-                    def _():
-                        copy.wait_send()
-
-                else:
-                    copy.wait_send()
+        for pi in range(2):
+            for ka in range(2):
+                cross(pi, ka).wait_send()
+        for ka in range(2):
+            for e in (0, 1, 3):
+                to_pair(ka, e).wait_send()
+
+        @pl.when(home)
+        def _():
+            for ka in range(2):
+                for e in (1, 3):
+                    to_near(ka, e, 0).wait_send()
+
+                @pl.when(k != ka)
+                def _():
+                    to_near(ka, 0, 0).wait_send()
+
+        @pl.when(away)
+        def _():
+            for ka in range(2):
+                for e in (0, 1, 3):
+                    to_near(ka, e, 1).wait_send()
 
 
 def on_device(factors, amplitudes, tile_mask):
@@ -356,15 +452,18 @@
             pltpu.VMEM((2, 2, 256, 1024), F32),
             pltpu.VMEM((2048, 512), BF),
             pltpu.VMEM((4, 512, 512), BF),
-            pltpu.VMEM((16, 512, 128), BF),
+            pltpu.VMEM((2, 2, 512, 128), BF),
+            pltpu.VMEM((6, 512, 128), BF),
+            pltpu.VMEM((9, 512, 128), BF),
             dma((16,)), dma((16,)), dma((2,)), dma((2,)), dma((2,)), dma((2,)),
             dma((18,)), dma((18,)), dma((18,)), dma((18,)), dma((18,)), dma((18,)),
-            dma((20,)), dma((20,)), dma((20,)), dma((20,)), dma((16,)), dma((16,)),
+            dma((20,)), dma((20,)), dma((20,)), dma((20,)),
+            dma((2, 2)), dma((2, 2)), dma((6,)), dma((6,)), dma((6,)), dma((9,)),
         ],
         compiler_params=pltpu.CompilerParams(
             collective_id=0, has_side_effects=True, vmem_limit_bytes=60 * 1024 * 1024
         ),
-    )(tile_mask.reshape(128), fl, fr, tt)
+    )(tile_mask.transpose(1, 2, 0), fl, fr, tt)
     return result.reshape(4, NB, 512)
 
 

time: 130 us -> 124 us (0.954)
  the two profiles are of different devices: /device:TPU:17 before, /device:TPU:1 now
where the time goes in v3:
time: 124 us; the launch traced here: 123 us
  Pallas kernels  114 us (92%)
  local copies, waits for them, and re-layouts  8.26 us (7%)
    pallas_call x1, Pallas kernels, on_device(): pl.pallas_call(kernel, name='ladder', out_shape=jax.ShapeDtypeStruct((256...  114 us

profile of v3, /device:TPU:1, one launch (start us, length us, event | category | flops | bytes accessed | tf_op | source)
XLA Modules:
  0.0 122.6 jit_solution(14157974604923657188)
XLA Ops:
  0.0 0.0 copy-start
  0.0 2.1 %copy.9 = bf16[32,64,128]{2,1,0:T(8,128)(2,1)} copy(bf16[32,64,128]{2,0,1:T(8,128)(2,1)} %bitcast.18) | data formatting | bytes 1048576 | tf_op jit(solution)/shard_map/transpose | solution.py:439
  2.1 0.0 copy-done
  2.1 1.1 copy.8
  3.3 1.0 copy.10.fr
  4.3 2.3 %copy.7 = bf16[128,32,128]{2,1,0:T(8,128)(2,1)} copy(bf16[128,32,128]{0,1,2:T(8,128)(2,1)S(1)} %bitcast.13) | data formatting | bytes 2097152 | tf_op jit(solution)/shard_map/transpose | solution.py:437
  6.6 114.3 %ladder.1 = bf16[256,512]{1,0:T(8,128)(2,1)} custom-call(s32[2,2,32]{2,1,0:T(2,128)} %bitcast.19, bf16[4,4,2,2,2,32,128]{6,5,4,3,2,1,0:T(8,128)(2,1)} %bitcast.14, bf16[2,8,128,128]{3,2,1,0:T(8,128)(2,1)} %copy.10.fr, bf16[2,16,64,128]{3,2,1,0:T(8,128)(2,1)} %bitcast.16), custom_call_target="tpu_custom_call" | custom-call | tf_op jit(solution)/shard_map/ladder/pallas_call | solution.py:442
  120.9 1.7 %copy.12 = bf16[4,64,512]{2,1,0:T(8,128)(2,1)} copy(bf16[4,64,512]{2,1,0:T(8,128)(2,1)} %bitcast.17) | data formatting | bytes 524288
Async XLA Ops:
  0.0 2.1 %copy-start = (bf16[128,32,128]{2,1,0:T(8,128)(2,1)S(1)}, bf16[128,32,128]{2,1,0:T(8,128)(2,1)}, u32[]{:S(2)}) copy-start(bf16[128,32,128]{2,1,0:T(8,128)(2,1)} %param.3) | copy-start | bytes 3145732

commit v4 on v3

--- a/solution.py
+++ b/solution.py
@@ -13,15 +13,15 @@
 F32 = jnp.float32
 SUBS = [(dz, dv, ac) for dz, dv in ((0, 0), (1, 0), (3, 0), (0, 1), (1, 1), (3, 1), (2, 0), (2, 1)) for ac in (0, 1)]
 SPANS = {(0, None): (0, 7), (0, 0): (0, 4), (0, 1): (4, 3), (1, None): (7, 9), (1, 0): (7, 4), (1, 1): (11, 5)}
-BLOCK_SPANS = {(0, None): (0, 7), (0, 0): (0, 2), (0, 1): (2, 5), (1, None): (7, 9), (1, 0): (7, 3), (1, 1): (10, 6)}
+BLOCK_SPANS = {(0, None): (0, 7), (0, 0): (0, 4), (0, 1): (4, 3), (1, None): (7, 9), (1, 0): (7, 4), (1, 1): (11, 5)}
 STEP = {0: 0, 1: 1, 3: 2}
 PLAN = (
-    "l4", "l0", "l1", "r4", "r0", "r1", "r9", "r10", "r11", "r3", "r2", "r5",
-    "r13", "r12", "TB", "l9", "l10", "l11", "r6", "r14", "r15", "r8", "l3", "l2",
-    "r7", "r16", "r17", "RS", "G00", "l5", "t0", "t1", "G10", "t4", "G03", "t10",
-    "t11", "l13", "l12", "t2", "t3", "t9", "l6", "G01", "t5", "G13", "l14", "l15",
-    "l8", "t14", "t15", "t12", "t13", "G11", "t6", "t7", "G02", "l7", "l16", "t8",
-    "l17", "t16", "t17", "G12", "TS",
+    "r0", "r1", "r9", "r4", "l4", "r10", "r11", "l0", "l1", "r3", "r2", "r5",
+    "r12", "r13", "TB", "l9", "r14", "r15", "r6", "l10", "l11", "r8", "r7", "l3",
+    "l2", "r16", "r17", "RS", "G00", "G10", "t0", "t1", "t9", "G03", "G01", "t4",
+    "t10", "t11", "l5", "l13", "l12", "l6", "t2", "t3", "G13", "G11", "t13", "t12",
+    "t5", "l14", "l15", "G02", "t6", "t14", "t15", "l8", "l7", "l16", "l17", "G12",
+    "t7", "t8", "t16", "t17", "TS",
 )
 
 
@@ -71,7 +71,8 @@
             self.sent.append(copy)
 
     def begin(self, part):
-        for e in ((0, 1, 4), (9, 10, 11))[part]:
+        both = self.sibling is not None
+        for e in ((0, 1) if both else (0, 1, 4), (9, 10, 11, 4) if both else (9, 10, 11))[part]:
             self._go(e)
         self._share(18 + part, (self.i, self.j, part, None))
 

time: 124 us -> 117 us (0.944)
  Pallas kernels: 114 us -> 108 us
    pallas_call x1, Pallas kernels: 114 us -> 108 us  [on_device(): pl.pallas_call(kernel, name='ladder', out_shape=jax.ShapeDtypeStruct((256...]
where the time goes in v4:
time: 117 us; the launch traced here: 116 us
  Pallas kernels  108 us (92%)
  local copies, waits for them, and re-layouts  8.26 us (7%)
    pallas_call x1, Pallas kernels, on_device(): pl.pallas_call(kernel, name='ladder', out_shape=jax.ShapeDtypeStruct((256...  108 us

profile of v4, /device:TPU:1, one launch (start us, length us, event | category | flops | bytes accessed | tf_op | source)
XLA Modules:
  0.0 116.4 jit_solution(11062288954335681098)
XLA Ops:
  0.0 0.0 copy-start
  0.0 2.1 %copy.9 = bf16[32,64,128]{2,1,0:T(8,128)(2,1)} copy(bf16[32,64,128]{2,0,1:T(8,128)(2,1)} %bitcast.18) | data formatting | bytes 1048576 | tf_op jit(solution)/shard_map/transpose | solution.py:440
  2.1 0.0 copy-done
  2.1 1.1 copy.8
  3.3 1.0 copy.10.fr
  4.3 2.3 %copy.7 = bf16[128,32,128]{2,1,0:T(8,128)(2,1)} copy(bf16[128,32,128]{0,1,2:T(8,128)(2,1)S(1)} %bitcast.13) | data formatting | bytes 2097152 | tf_op jit(solution)/shard_map/transpose | solution.py:438
  6.6 108.2 %ladder.1 = bf16[256,512]{1,0:T(8,128)(2,1)} custom-call(s32[2,2,32]{2,1,0:T(2,128)} %bitcast.19, bf16[4,4,2,2,2,32,128]{6,5,4,3,2,1,0:T(8,128)(2,1)} %bitcast.14, bf16[2,8,128,128]{3,2,1,0:T(8,128)(2,1)} %copy.10.fr, bf16[2,16,64,128]{3,2,1,0:T(8,128)(2,1)} %bitcast.16), custom_call_target="tpu_custom_call" | custom-call | tf_op jit(solution)/shard_map/ladder/pallas_call | solution.py:443
  114.8 1.7 %copy.12 = bf16[4,64,512]{2,1,0:T(8,128)(2,1)} copy(bf16[4,64,512]{2,1,0:T(8,128)(2,1)} %bitcast.17) | data formatting | bytes 524288
Async XLA Ops:
  0.0 2.1 %copy-start = (bf16[128,32,128]{2,1,0:T(8,128)(2,1)S(1)}, bf16[128,32,128]{2,1,0:T(8,128)(2,1)}, u32[]{:S(2)}) copy-start(bf16[128,32,128]{2,1,0:T(8,128)(2,1)} %param.3) | copy-start | bytes 3145732

commit v5 on v4

--- a/solution.py
+++ b/solution.py
@@ -11,8 +11,9 @@
 NB = 64
 BF = jnp.bfloat16
 F32 = jnp.float32
+VMEM_MIB = 48
 SUBS = [(dz, dv, ac) for dz, dv in ((0, 0), (1, 0), (3, 0), (0, 1), (1, 1), (3, 1), (2, 0), (2, 1)) for ac in (0, 1)]
-SPANS = {(0, None): (0, 7), (0, 0): (0, 4), (0, 1): (4, 3), (1, None): (7, 9), (1, 0): (7, 4), (1, 1): (11, 5)}
+SPANS = {(0, None): (0, 8), (0, 0): (0, 4), (0, 1): (4, 4), (1, None): (8, 8), (1, 0): (8, 4), (1, 1): (12, 4)}
 BLOCK_SPANS = {(0, None): (0, 7), (0, 0): (0, 4), (0, 1): (4, 3), (1, None): (7, 9), (1, 0): (7, 4), (1, 1): (11, 5)}
 STEP = {0: 0, 1: 1, 3: 2}
 PLAN = (
@@ -20,8 +21,8 @@
     "r12", "r13", "TB", "l9", "r14", "r15", "r6", "l10", "l11", "r8", "r7", "l3",
     "l2", "r16", "r17", "RS", "G00", "G10", "t0", "t1", "t9", "G03", "G01", "t4",
     "t10", "t11", "l5", "l13", "l12", "l6", "t2", "t3", "G13", "G11", "t13", "t12",
-    "t5", "l14", "l15", "G02", "t6", "t14", "t15", "l8", "l7", "l16", "l17", "G12",
-    "t7", "t8", "t16", "t17", "TS",
+    "t5", "l14", "l15", "G02", "t6", "t14", "t15", "l8", "l7", "l16", "l17", "t7",
+    "t8", "t16", "t17", "G12", "TS",
 )
 
 
@@ -98,8 +99,9 @@
 
 
 def kernel(
-    mask, fl, fr, tt, out,
+    mask, fl, factors, amplitudes, out,
     lb, rb, tb, gr, w, pb, m1, m2, rs,
+    f32s, t32s, fr, tt,
     la_s, la_r, ra_s, ra_r, ta_s, ta_r,
     lg_s, lg_r, rg_s, rg_r, tg_s, tg_r,
     rd_s, rd_r, td_s, td_r, m1_s, m1_r, far_s, m2_r, near_s, rs_r,
@@ -130,6 +132,26 @@
                                 device_id_type=MESH,
                             )
                             count += 1
+
+    with jax.named_scope("prep_r"):
+        low_q = lax.broadcasted_iota(jnp.int32, (128, 128), 1) < 64
+
+        def widen(n, carry):
+            rows = pl.ds(pl.multiple_of(n * 512, 512), 512)
+            f32s[rows, :] = factors[pl.ds(n * 16, 16)].astype(F32).reshape(512, 128)
+            return carry
+
+        lax.fori_loop(0, 8, widen, 0)
+
+        def pair_up(n, carry):
+            even = f32s[pl.ds(2 * n, 128, stride=32), :]
+            odd = f32s[pl.ds(2 * n + 1, 128, stride=32), :]
+            fr[n] = jnp.where(low_q, even, pltpu.roll(odd, 64, 1)).astype(BF)
+            return carry
+
+        lax.fori_loop(0, 16, pair_up, 0)
+
+    with jax.named_scope("barrier_wait"):
         pl.semaphore_wait(barrier, count)
 
     yhi, ylo = y // 2, lax.rem(y, 2)
@@ -140,15 +162,17 @@
             y_to = 2 * k + dl
             here = dst.at[z, xl, pl.ds(y * depth, depth)]
 
+            part = src.at[pl.ds(dl * depth, depth)]
+
             @pl.when(y_to == y)
             def _():
-                pltpu.make_async_copy(src.at[dl], here, rr.at[ylo]).start()
+                pltpu.make_async_copy(part, here, rr.at[ylo]).start()
 
             @pl.when(y_to != y)
             def _():
-                remote(src.at[dl], here, ss.at[dl], rr.at[ylo], dev(xh, yhi, z, y_to, xl)).start()
-
-            routed.append((src.at[dl], here, ss.at[dl], rr.at[ylo], y_to))
+                remote(part, here, ss.at[dl], rr.at[ylo], dev(xh, yhi, z, y_to, xl)).start()
+
+            routed.append((part, here, ss.at[dl], rr.at[ylo], y_to))
 
     left = []
     with jax.named_scope("issue"):
@@ -224,6 +248,16 @@
 
         lax.fori_loop(0, 4, step, 0)
 
+    with jax.named_scope("prep_t"):
+        for n in range(4):
+            t32s[n * 512 : n * 512 + 512, :] = amplitudes[n * 16 : n * 16 + 16].astype(F32).reshape(512, 128)
+
+        def major_d(n, carry):
+            tt[n] = t32s[pl.ds(n, 64, stride=32), :].astype(BF)
+            return carry
+
+        lax.fori_loop(0, 32, major_d, 0)
+
     with jax.named_scope("own_r"):
         own_arrived(rb, ra_s, ra_r, 8, 0)
         rg.begin(0)
@@ -231,11 +265,11 @@
         rg.begin(1)
         route(tt, tb, ta_s, ta_r, 16)
     with jax.named_scope("own_l"):
-        for n in range(7):
+        for n in range(8):
             left_arrived(n)
         lg.begin(0)
     with jax.named_scope("own_lb"):
-        for n in range(7, 16):
+        for n in range(8, 16):
             left_arrived(n)
         lg.begin(1)
     gathers = {"l": lg, "r": rg, "t": tg}
@@ -288,10 +322,6 @@
         def _():
             to_pair(ka, e).start()
 
-        @pl.when(away)
-        def _():
-            to_far(ka, e).start()
-
     def send_home(ka, e):
         if e != 0:
             to_near(ka, e, 0).start()
@@ -371,6 +401,8 @@
         def _():
             take_pair(0, 0)
             take_pair(0, 3)
+            for ka, e in ((0, 0), (0, 3), (1, 0), (1, 1)):
+                to_far(ka, e).start()
             for ka in range(2):
                 to_far(ka, take_cross(1 - xh, ka)).start()
             take_pair(1, 0)
@@ -436,16 +468,14 @@
 
 def on_device(factors, amplitudes, tile_mask):
     fl = factors.transpose(2, 1, 0).reshape(4, 4, 2, 2, 2, 32, 128)
-    fr = factors[:, :, :NB].reshape(128, 2, 8, 2, NB).transpose(1, 2, 0, 3, 4).reshape(2, 8, 128, 128)
-    tt = amplitudes.transpose(1, 0, 2).reshape(2, 16, 64, 128)
     dma = pltpu.SemaphoreType.DMA
-    any_space = pl.BlockSpec(memory_space=pl.ANY)
+    vmem_space = pl.BlockSpec(memory_space=pltpu.VMEM)
     result = pl.pallas_call(
         kernel,
         name="ladder",
         out_shape=jax.ShapeDtypeStruct((256, 512), BF),
-        in_specs=[pl.BlockSpec(memory_space=pltpu.SMEM)] + [any_space] * 3,
-        out_specs=pl.BlockSpec(memory_space=pltpu.VMEM),
+        in_specs=[pl.BlockSpec(memory_space=pltpu.SMEM)] + [pl.BlockSpec(memory_space=pl.ANY), vmem_space, vmem_space],
+        out_specs=vmem_space,
         scratch_shapes=[
             pltpu.VMEM((2, 4, 16, 4, 2, 32, 128), BF),
             pltpu.VMEM((4, 2, 32, 128, 128), BF),
@@ -456,15 +486,19 @@
             pltpu.VMEM((2, 2, 512, 128), BF),
             pltpu.VMEM((6, 512, 128), BF),
             pltpu.VMEM((9, 512, 128), BF),
+            pltpu.VMEM((4096, 128), F32),
+            pltpu.VMEM((2048, 128), F32),
+            pltpu.VMEM((16, 128, 128), BF),
+            pltpu.VMEM((32, 64, 128), BF),
             dma((16,)), dma((16,)), dma((2,)), dma((2,)), dma((2,)), dma((2,)),
             dma((18,)), dma((18,)), dma((18,)), dma((18,)), dma((18,)), dma((18,)),
             dma((20,)), dma((20,)), dma((20,)), dma((20,)),
             dma((2, 2)), dma((2, 2)), dma((6,)), dma((6,)), dma((6,)), dma((9,)),
         ],
         compiler_params=pltpu.CompilerParams(
-            collective_id=0, has_side_effects=True, vmem_limit_bytes=60 * 1024 * 1024
+            collective_id=0, has_side_effects=True, vmem_limit_bytes=VMEM_MIB * 1024 * 1024
         ),
-    )(tile_mask.transpose(1, 2, 0), fl, fr, tt)
+    )(tile_mask.transpose(1, 2, 0), fl, factors, amplitudes)
     return result.reshape(4, NB, 512)
 
 

time: 117 us -> 107 us (0.915)
  Pallas kernels: 108 us -> 103 us
  local copies, waits for them, and re-layouts: 8.26 us -> 3.31 us
    pallas_call x1, Pallas kernels: 108 us -> 103 us  [on_device(): pl.pallas_call(kernel, name='ladder', out_shape=jax.ShapeDtypeStruct((256...]
    transpose x1 -> x0, local copies, waits for them, and re-layouts: 2.14 us -> none  [on_device(): tt = amplitudes.transpose(1, 0, 2).reshape(2, 16, 64, 128)]
where the time goes in v5:
time: 107 us
  Pallas kernels  103 us (96%)
  local copies, waits for them, and re-layouts  3.31 us (3%)
    pallas_call x1, Pallas kernels, on_device(): pl.pallas_call(kernel, name='ladder', out_shape=jax.ShapeDtypeStruct((256...  103 us
    transpose x1, local copies, waits for them, and re-layouts, on_device(): fl = factors.transpose(2, 1, 0).reshape(4, 4, 2, 2, 2, 32, 128)  2.59 us

profile of v5, /device:TPU:1, one launch (start us, length us, event | category | flops | bytes accessed | tf_op | source)
XLA Modules:
  0.0 106.8 jit_solution(15066158329214408728)
XLA Ops:
  0.0 0.0 copy-start
  0.0 0.0 copy-start.1
  0.0 0.0 copy-start.2
  0.0 2.6 %copy.4 = bf16[128,32,128]{2,1,0:T(8,128)(2,1)S(1)} copy(bf16[128,32,128]{0,1,2:T(8,128)(2,1)} %bitcast.4) | data formatting | bytes 2097152 | tf_op jit(solution)/shard_map/transpose | solution.py:470
  2.6 0.0 copy-done
  2.6 0.0 copy-done.1
  2.6 0.0 copy-done.2
  2.6 103.4 %ladder.1 = bf16[256,512]{1,0:T(8,128)(2,1)S(1)} custom-call(s32[2,2,32]{2,1,0:T(2,128)S(1)} %bitcast.7, bf16[4,4,2,2,2,32,128]{6,5,4,3,2,1,0:T(8,128)(2,1)S(1)} %bitcast.5, bf16[128,32,128]{2,1,0:T(8,128)(2,1)S(1)} %copy-done, bf16[64,32,128]{2,1,0:T(8,128)(2,1)S(1)} %copy-done.1), custom_call_target="tpu_custom_call" | custom-call | tf_op jit(solution)/shard_map/ladder/pallas_call | solution.py:473
  106.1 0.7 copy.6
Async XLA Ops:
  0.0 2.6 %copy-start = (bf16[128,32,128]{2,1,0:T(8,128)(2,1)S(1)}, bf16[128,32,128]{2,1,0:T(8,128)(2,1)}, u32[]{:S(2)}) copy-start(bf16[128,32,128]{2,1,0:T(8,128)(2,1)} %factors.1) | copy-start | bytes 3145732
  0.0 2.6 %copy-start.1 = (bf16[64,32,128]{2,1,0:T(8,128)(2,1)S(1)}, bf16[64,32,128]{2,1,0:T(8,128)(2,1)}, u32[]{:S(2)}) copy-start(bf16[64,32,128]{2,1,0:T(8,128)(2,1)} %amplitudes.1) | copy-start | bytes 1572868
  0.0 2.6 %copy-start.2 = (s32[32,2,2]{0,2,1:T(2,128)S(1)}, s32[32,2,2]{0,2,1:T(2,128)}, u32[]{:S(2)}) copy-start(s32[32,2,2]{0,2,1:T(2,128)} %param.5) | copy-start | bytes 1540

commit v6 on v5

--- a/solution.py
+++ b/solution.py
@@ -13,11 +13,12 @@
 F32 = jnp.float32
 VMEM_MIB = 48
 SUBS = [(dz, dv, ac) for dz, dv in ((0, 0), (1, 0), (3, 0), (0, 1), (1, 1), (3, 1), (2, 0), (2, 1)) for ac in (0, 1)]
-SPANS = {(0, None): (0, 8), (0, 0): (0, 4), (0, 1): (4, 4), (1, None): (8, 8), (1, 0): (8, 4), (1, 1): (12, 4)}
+SPANS = {(0, None): (0, 7), (0, 0): (0, 4), (0, 1): (4, 3), (1, None): (7, 9), (1, 0): (7, 4), (1, 1): (11, 5)}
+FIRST, PART = 4, 7
 BLOCK_SPANS = {(0, None): (0, 7), (0, 0): (0, 4), (0, 1): (4, 3), (1, None): (7, 9), (1, 0): (7, 4), (1, 1): (11, 5)}
 STEP = {0: 0, 1: 1, 3: 2}
 PLAN = (
-    "r0", "r1", "r9", "r4", "l4", "r10", "r11", "l0", "l1", "r3", "r2", "r5",
+    "r0", "r1", "r9", "r4", "l18", "l4", "r10", "r11", "l0", "l1", "r3", "r2", "r5",
     "r12", "r13", "TB", "l9", "r14", "r15", "r6", "l10", "l11", "r8", "r7", "l3",
     "l2", "r16", "r17", "RS", "G00", "G10", "t0", "t1", "t9", "G03", "G01", "t4",
     "t10", "t11", "l5", "l13", "l12", "l6", "t2", "t3", "G13", "G11", "t13", "t12",
@@ -38,7 +39,6 @@
         self.pair = pair
         self.send, self.recv = send, recv
         self.sibling = sibling
-        self.sent = []
         i1, i2, i3, o = lax.rem(i + 1, 4), lax.rem(i + 2, 4), lax.rem(i + 3, 4), 1 - j
         self.brings = [
             (i3, j, 0, None), (i1, j, 0, None), (i2, j, 0, 0), (i2, j, 0, 1),
@@ -54,48 +54,47 @@
             ((i, j, 1, None), up), ((i, j, 1, None), down), ((i, o, 1, None), up), ((i, o, 1, None), down),
             ((i3, j, 1, 0), up), ((i1, j, 1, 1), down), ((i3, o, 1, 0), up), ((i1, o, 1, 1), down),
         ]
+        if sibling is None:
+            self.brings[4], self.sends[4] = (i, o, 0, 1), ((i, j, 0, 1), pair)
+            self.brings.append((i, o, 0, 0))
+            self.sends.append(((i, j, 0, 0), pair))
         self.then = {0: (2, 5), 1: (3, 6), 2: (7,), 3: (8,), 9: (12, 13), 10: (14,), 11: (15,), 12: (16,), 13: (17,)}
 
     def _go(self, e):
         where, dev = self.sends[e]
         ref = self.piece(*where)
-        copy = remote(ref, ref, self.send.at[e], self.recv.at[e], dev)
-        copy.start()
-        self.sent.append(copy)
-
-    def _share(self, slot, where):
+        remote(ref, ref, self.send.at[0], self.recv.at[e], dev).start()
+
+    def _share(self, where):
         if self.sibling is not None:
             dev, send, recv = self.sibling
             ref = self.piece(*where)
-            copy = remote(ref, ref, send.at[slot], recv.at[slot], dev)
-            copy.start()
-            self.sent.append(copy)
+            remote(ref, ref, send.at[0], recv.at[0], dev).start()
 
     def begin(self, part):
         both = self.sibling is not None
         for e in ((0, 1) if both else (0, 1, 4), (9, 10, 11, 4) if both else (9, 10, 11))[part]:
             self._go(e)
-        self._share(18 + part, (self.i, self.j, part, None))
+        self._share((self.i, self.j, part, None))
 
     def event(self, e):
         with jax.named_scope(self.name + str(e)):
             ref = self.piece(*self.brings[e])
-            remote(ref, ref, self.send.at[e], self.recv.at[e], self.pair).wait_recv()
+            remote(ref, ref, self.send.at[0], self.recv.at[e], self.pair).wait_recv()
             for s in self.then.get(e, ()):
                 self._go(s)
-            self._share(e, self.brings[e])
-
-    def sibling_wait(self, other_piece):
+            self._share(self.brings[e])
+
+    def sibling_wait(self, others):
         dev, send, recv = self.sibling
         with jax.named_scope(self.name + "_sib"):
-            for slot in range(20):
-                where = self.brings[slot] if slot < 18 else (self.i, self.j, slot - 18, None)
-                ref = other_piece(*where)
-                remote(ref, ref, send.at[slot], recv.at[slot], dev).wait_recv()
-
-    def finish(self):
-        for copy in self.sent:
-            copy.wait_send()
+            remote(others, others, send.at[0], recv.at[0], dev).wait_recv()
+
+    def finish(self, seven, eight=None):
+        remote(seven, seven, self.send.at[0], self.recv.at[0], self.pair).wait_send()
+        if eight is not None:
+            dev, send, recv = self.sibling
+            remote(eight, eight, send.at[0], recv.at[0], dev).wait_send()
 
 
 def kernel(
@@ -160,7 +159,7 @@
     def route(src, dst, ss, rr, depth):
         for dl in range(2):
             y_to = 2 * k + dl
-            here = dst.at[z, xl, pl.ds(y * depth, depth)]
+            here = dst.at[z * 2 + xl, pl.ds(y * depth, depth)]
 
             part = src.at[pl.ds(dl * depth, depth)]
 
@@ -174,28 +173,26 @@
 
             routed.append((part, here, ss.at[dl], rr.at[ylo], y_to))
 
-    left = []
     with jax.named_scope("issue"):
         for n, (dz, dv, ac) in enumerate(SUBS):
             z_to, v_to, k_to = lax.rem(z + dz, 4), lax.rem(v + dv, 2), lax.rem(k + ac, 2)
-            src, here = fl.at[z_to, :, k_to, v_to], lb.at[xh, y, n]
+            src, here = fl.at[z_to, :, k_to, v_to], lb.at[xh * 4 + y, n]
             if n == 0:
-                pltpu.make_async_copy(src, here, la_r.at[n]).start()
+                pltpu.make_async_copy(src, here, la_r.at[0]).start()
             else:
-                copy = remote(src, here, la_s.at[n], la_r.at[n], dev(xh, k_to, z_to, y, lax.rem(xl + dv, 2)))
-                copy.start()
-                left.append(copy)
+                group = 0 if n < FIRST else 1 if n < PART else 2
+                remote(src, here, la_s.at[0], la_r.at[group], dev(xh, k_to, z_to, y, lax.rem(xl + dv, 2))).start()
             if n == 3:
                 route(fr, rb, ra_s, ra_r, 8)
 
     def l_piece(i, j, part, half):
         first, some = SPANS[part, half]
-        return lb.at[j, i, pl.ds(first, some)]
+        return lb.at[j * 4 + i, pl.ds(first, some)]
 
     def block_piece(buf, scale, core):
         def piece(i, j, part, half):
             first, some = BLOCK_SPANS[part, half]
-            return buf.at[i, j, pl.ds((core * 16 + first) * scale, some * scale)]
+            return buf.at[i * 2 + j, pl.ds((core * 16 + first) * scale, some * scale)]
 
         return piece
 
@@ -208,12 +205,13 @@
     tg = Gather("t", block_piece(tb, 2, k), z, xl, z_up, z_down, v_pair, tg_s, tg_r, (sib, td_s, td_r))
 
     def own_arrived(dst, ss, rr, depth, n):
-        ref = dst.at[z, xl, pl.ds((2 * k + n) * depth, depth)]
+        ref = dst.at[z * 2 + xl, pl.ds((2 * k + n) * depth, depth)]
         remote(ref, ref, ss.at[n], rr.at[n], sib).wait_recv()
 
-    def left_arrived(n):
-        ref = lb.at[xh, y, n]
-        remote(ref, ref, la_s.at[n], la_r.at[n], sib).wait_recv()
+    def left_arrived(group):
+        first, last = ((0, FIRST), (FIRST, PART), (PART, 16))[group]
+        ref = lb.at[xh * 4 + y, pl.ds(first, last - first)]
+        remote(ref, ref, la_s.at[0], la_r.at[group], sib).wait_recv()
 
     def gram(h_rel, dy, place):
         h, yy = lax.rem(xh + h_rel, 2), lax.rem(y + dy, 4)
@@ -222,13 +220,20 @@
             rhs = []
             for dz, dv, ac in SUBS[::2]:
                 zz, x = lax.rem(z - dz + 4, 4), lax.rem(xl + xh + dv + h, 2)
-                rhs.append(jnp.concatenate([rb[zz, x, yy * 8 + 2 * n], rb[zz, x, yy * 8 + 2 * n + 1]], axis=1))
+                rhs.append(jnp.concatenate([rb[zz * 2 + x, yy * 8 + 2 * n], rb[zz * 2 + x, yy * 8 + 2 * n + 1]], axis=1))
             rhs = jnp.concatenate(rhs, axis=0)
             col = pl.ds(pl.multiple_of(n * 256, 256), 256)
             low = lax.broadcasted_iota(jnp.int32, (32, 128), 1) < 64
+            lhs = jnp.concatenate(
+                [
+                    jnp.concatenate([lb[h * 4 + yy, 2 * s + ac].reshape(256, 128) for s in range(8)], axis=1)
+                    for ac in range(2)
+                ],
+                axis=0,
+            )
+            both = jnp.dot(lhs, rhs, preferred_element_type=F32)
             for ac in range(2):
-                lhs = jnp.concatenate([lb[h, yy, 2 * s + ac].reshape(256, 128) for s in range(8)], axis=1)
-                got = jnp.dot(lhs, rhs, preferred_element_type=F32)
+                got = both[ac * 256 : ac * 256 + 256]
                 if place != "first":
                     got = got + gr[h_rel, ac, :, col]
                 if place != "last":
@@ -258,19 +263,20 @@
 
         lax.fori_loop(0, 32, major_d, 0)
 
+    with jax.named_scope("own_l"):
+        left_arrived(0)
+        lg._go(18)
+    with jax.named_scope("own_l2"):
+        left_arrived(1)
+        lg.begin(0)
     with jax.named_scope("own_r"):
         own_arrived(rb, ra_s, ra_r, 8, 0)
         rg.begin(0)
         own_arrived(rb, ra_s, ra_r, 8, 1)
         rg.begin(1)
         route(tt, tb, ta_s, ta_r, 16)
-    with jax.named_scope("own_l"):
-        for n in range(8):
-            left_arrived(n)
-        lg.begin(0)
     with jax.named_scope("own_lb"):
-        for n in range(8, 16):
-            left_arrived(n)
+        left_arrived(2)
         lg.begin(1)
     gathers = {"l": lg, "r": rg, "t": tg}
     for word in PLAN:
@@ -281,9 +287,9 @@
                 own_arrived(tb, ta_s, ta_r, 16, 1)
                 tg.begin(1)
         elif word == "RS":
-            rg.sibling_wait(block_piece(rb, 1, 1 - k))
+            rg.sibling_wait(rb.at[:, pl.ds((1 - k) * 16, 16)])
         elif word == "TS":
-            tg.sibling_wait(block_piece(tb, 2, 1 - k))
+            tg.sibling_wait(tb.at[:, pl.ds((1 - k) * 32, 32)])
         elif word[0] == "G":
             place = "last" if word[2] == "2" else "first" if word[2] == "0" else "more"
             with jax.named_scope(word):
@@ -338,19 +344,16 @@
     def ladder(qt):
         low = lax.broadcasted_iota(jnp.int32, (1, 128), 1) < 64
 
-        def rows(m, carry):
+        def rows(half, carry):
             lhs = []
-            for yy in range(2):
+            for yyy in range(4):
                 for x in range(2):
-                    yyy = 2 * m + yy
                     block = qt * 8 + yyy * 2 + x
                     keep = jnp.where(low, mask[0, xh, block], mask[1, xh, block]).astype(F32).astype(BF)
-                    lhs.append(jnp.concatenate([tb[qt, x, yyy * 16 + dd] * keep for dd in range(16)], axis=1))
+                    lhs.append(jnp.concatenate([tb[qt * 2 + x, yyy * 16 + dd] * keep for dd in range(16)], axis=1))
             lhs = jnp.concatenate(lhs, axis=0)
-            at = pl.ds(pl.multiple_of(m * 256, 256), 256)
-            for half in range(2):
-                got = jnp.dot(lhs, w[:, half * 256 : half * 256 + 256], preferred_element_type=F32)
-                pb[qt, at, half * 256 : half * 256 + 256] = got.astype(BF)
+            at = pl.ds(pl.multiple_of(half * 256, 256), 256)
+            pb[qt, :, at] = jnp.dot(lhs, w[:, at], preferred_element_type=F32).astype(BF)
             return carry
 
         lax.fori_loop(0, 2, rows, 0)
@@ -419,28 +422,30 @@
             def _():
                 remote(src, here, ss, rr, sib).wait_send()
 
-        for copy in left:
-            copy.wait_send()
-        lg.finish()
-        rg.finish()
-        tg.finish()
-
-    def gathered(slots):
-        total = None
+        ref = lb.at[0, pl.ds(0, 15)]
+        remote(ref, ref, la_s.at[0], la_r.at[0], sib).wait_send()
+        lg.finish(lb.at[pl.ds(0, 7)])
+        rg.finish(rb.at[pl.ds(0, 7), pl.ds(0, 16)], rb.at[:, pl.ds(0, 16)])
+        tg.finish(tb.at[pl.ds(0, 7), pl.ds(0, 32)], tb.at[:, pl.ds(0, 32)])
+
+    for half, slots in ((1 - v, (3, 4, 5)), (v, (0, 1, 2, 6, 7, 8))):
         for n in slots:
             ref = rs.at[n]
             with jax.named_scope("rs%d" % n):
                 remote(ref, ref, near_s.at[0], rs_r.at[n], sib).wait_recv()
-            part = rs[n].astype(F32)
-            total = part if total is None else total + part
-        return total.T
-
-    for half, slots in ((v, (0, 6, 1, 2, 7, 8)), (1 - v, (3, 4, 5))):
-        total = gathered(slots)
-        at = pl.ds(pl.multiple_of(half * 128, 128), 128)
-        for m in range(8):
-            keep = mask[z // 2, 0, g * 8 + m].astype(F32)
-            out[at, m * 64 : m * 64 + 64] = (total[:, m * 64 : m * 64 + 64] * keep).astype(BF)
+
+        def total(m, carry):
+            cut = pl.ds(pl.multiple_of(m * 128, 128), 128)
+            got = rs[slots[0], cut, :].astype(F32)
+            for n in slots[1:]:
+                got = got + rs[n, cut, :].astype(F32)
+            block = g * 8 + 2 * m
+            low = lax.broadcasted_iota(jnp.int32, (1, 128), 1) < 64
+            keep = jnp.where(low, mask[z // 2, 0, block], mask[z // 2, 0, block + 1]).astype(F32)
+            out[pl.ds(pl.multiple_of(half * 128, 128), 128), cut] = (got.T * keep).astype(BF)
+            return carry
+
+        lax.fori_loop(0, 4, total, 0)
     with jax.named_scope("drain2"):
         for pi in range(2):
             for ka in range(2):
@@ -477,9 +482,9 @@
         in_specs=[pl.BlockSpec(memory_space=pltpu.SMEM)] + [pl.BlockSpec(memory_space=pl.ANY), vmem_space, vmem_space],
         out_specs=vmem_space,
         scratch_shapes=[
-            pltpu.VMEM((2, 4, 16, 4, 2, 32, 128), BF),
-            pltpu.VMEM((4, 2, 32, 128, 128), BF),
-            pltpu.VMEM((4, 2, 64, 64, 128), BF),
+            pltpu.VMEM((8, 16, 4, 2, 32, 128), BF),
+            pltpu.VMEM((8, 32, 128, 128), BF),
+            pltpu.VMEM((8, 64, 64, 128), BF),
             pltpu.VMEM((2, 2, 256, 1024), F32),
             pltpu.VMEM((2048, 512), BF),
             pltpu.VMEM((4, 512, 512), BF),
@@ -490,9 +495,9 @@
             pltpu.VMEM((2048, 128), F32),
             pltpu.VMEM((16, 128, 128), BF),
             pltpu.VMEM((32, 64, 128), BF),
-            dma((16,)), dma((16,)), dma((2,)), dma((2,)), dma((2,)), dma((2,)),
-            dma((18,)), dma((18,)), dma((18,)), dma((18,)), dma((18,)), dma((18,)),
-            dma((20,)), dma((20,)), dma((20,)), dma((20,)),
+            dma((1,)), dma((3,)), dma((2,)), dma((2,)), dma((2,)), dma((2,)),
+            dma((1,)), dma((19,)), dma((1,)), dma((18,)), dma((1,)), dma((18,)),
+            dma((1,)), dma((1,)), dma((1,)), dma((1,)),
             dma((2, 2)), dma((2, 2)), dma((6,)), dma((6,)), dma((6,)), dma((9,)),
         ],
         compiler_params=pltpu.CompilerParams(

time: 107 us -> 105 us (0.981)
    pallas_call x1, Pallas kernels: 103 us -> 102 us  [on_device(): pl.pallas_call(kernel, name='ladder', out_shape=jax.ShapeDtypeStruct((256...]
where the time goes in v6:
time: 105 us
  Pallas kernels  102 us (97%)
  local copies, waits for them, and re-layouts  3.31 us (3%)
    pallas_call x1, Pallas kernels, on_device(): pl.pallas_call(kernel, name='ladder', out_shape=jax.ShapeDtypeStruct((256...  102 us
    transpose x1, local copies, waits for them, and re-layouts, on_device(): fl = factors.transpose(2, 1, 0).reshape(4, 4, 2, 2, 2, 32, 128)  2.59 us

profile of v6, /device:TPU:1, one launch (start us, length us, event | category | flops | bytes accessed | tf_op | source)
XLA Modules:
  0.0 104.9 jit_solution(12022558961584124904)
XLA Ops:
  0.0 0.0 copy-start
  0.0 0.0 copy-start.1
  0.0 0.0 copy-start.2
  0.0 2.6 %copy.4 = bf16[128,32,128]{2,1,0:T(8,128)(2,1)S(1)} copy(bf16[128,32,128]{0,1,2:T(8,128)(2,1)} %bitcast.4) | data formatting | bytes 2097152 | tf_op jit(solution)/shard_map/transpose | solution.py:475
  2.6 0.0 copy-done
  2.6 0.0 copy-done.1
  2.6 0.0 copy-done.2
  2.6 101.5 %ladder.1 = bf16[256,512]{1,0:T(8,128)(2,1)S(1)} custom-call(s32[2,2,32]{2,1,0:T(2,128)S(1)} %bitcast.7, bf16[4,4,2,2,2,32,128]{6,5,4,3,2,1,0:T(8,128)(2,1)S(1)} %bitcast.5, bf16[128,32,128]{2,1,0:T(8,128)(2,1)S(1)} %copy-done, bf16[64,32,128]{2,1,0:T(8,128)(2,1)S(1)} %copy-done.1), custom_call_target="tpu_custom_call" | custom-call | tf_op jit(solution)/shard_map/ladder/pallas_call | solution.py:478
  104.2 0.7 copy.6
Async XLA Ops:
  0.0 2.6 %copy-start = (bf16[128,32,128]{2,1,0:T(8,128)(2,1)S(1)}, bf16[128,32,128]{2,1,0:T(8,128)(2,1)}, u32[]{:S(2)}) copy-start(bf16[128,32,128]{2,1,0:T(8,128)(2,1)} %factors.1) | copy-start | bytes 3145732
  0.0 2.6 %copy-start.1 = (bf16[64,32,128]{2,1,0:T(8,128)(2,1)S(1)}, bf16[64,32,128]{2,1,0:T(8,128)(2,1)}, u32[]{:S(2)}) copy-start(bf16[64,32,128]{2,1,0:T(8,128)(2,1)} %amplitudes.1) | copy-start | bytes 1572868
  0.0 2.6 %copy-start.2 = (s32[32,2,2]{0,2,1:T(2,128)S(1)}, s32[32,2,2]{0,2,1:T(2,128)}, u32[]{:S(2)}) copy-start(s32[32,2,2]{0,2,1:T(2,128)} %param.5) | copy-start | bytes 1540

commit v7 on v6

--- a/solution.py
+++ b/solution.py
@@ -305,23 +305,23 @@
         return pb.at[2 * pi + ka, :, pl.ds(pl.multiple_of(ya * 128, 128), 128)]
 
     def cross(pi, ka):
-        return remote(p_piece(pi, ka, 2), m1.at[ka, pi], m1_s.at[ka, pi], m1_r.at[ka, pi], (y_up, y_down)[ka])
+        return remote(p_piece(pi, ka, 2), m1.at[ka, pi], m1_s.at[0], m1_r.at[ka, pi], (y_up, y_down)[ka])
 
     def to_pair(ka, e):
         n = ka * 3 + STEP[e]
-        return remote(p_piece(1 - xh, ka, e), m2.at[n], far_s.at[n], m2_r.at[n], u_pair)
+        return remote(p_piece(1 - xh, ka, e), m2.at[n], far_s.at[0], m2_r.at[n], u_pair)
 
     def to_far(ka, e):
         n = ka * 3 + STEP[e]
         slot = 6 + STEP[e]
         owner = dev(1 - xh, ka, z, lax.rem(y + e, 4), 1 - xl)
-        return remote(p_piece(1 - xh, ka, e), rs.at[slot], far_s.at[n], rs_r.at[slot], owner)
+        return remote(p_piece(1 - xh, ka, e), rs.at[slot], far_s.at[0], rs_r.at[slot], owner)
 
     def to_near(ka, e, kind):
         n = ka * 3 + STEP[e]
         slot = 3 * kind + STEP[e]
         owner = dev(xh, ka, z, lax.rem(y + e, 4), (xl, 1 - xl)[kind])
-        return remote(p_piece(xh, ka, e), rs.at[slot], near_s.at[n], rs_r.at[slot], owner)
+        return remote(p_piece(xh, ka, e), rs.at[slot], near_s.at[0], rs_r.at[slot], owner)
 
     def send_far(ka, e):
         @pl.when(home)
@@ -380,14 +380,14 @@
     def take_cross(pi, ka):
         e = (1, 3)[ka]
         ref = m1.at[ka, pi]
-        remote(ref, ref, m1_s.at[ka, pi], m1_r.at[ka, pi], sib).wait_recv()
+        remote(ref, ref, m1_s.at[0], m1_r.at[ka, pi], sib).wait_recv()
         merge(pi, ka, e, ref)
         return e
 
     def take_pair(ka, e):
         n = ka * 3 + STEP[e]
         ref = m2.at[n]
-        remote(ref, ref, far_s.at[n], m2_r.at[n], sib).wait_recv()
+        remote(ref, ref, far_s.at[0], m2_r.at[n], sib).wait_recv()
         merge(xh, ka, e, ref)
         to_near(ka, e, 1).start()
 
@@ -447,28 +447,18 @@
 
         lax.fori_loop(0, 4, total, 0)
     with jax.named_scope("drain2"):
-        for pi in range(2):
-            for ka in range(2):
-                cross(pi, ka).wait_send()
-        for ka in range(2):
-            for e in (0, 1, 3):
-                to_pair(ka, e).wait_send()
+        remote(m1, m1, m1_s.at[0], m1_r.at[0, 0], sib).wait_send()
+        remote(m2, m2, far_s.at[0], m2_r.at[0], sib).wait_send()
 
         @pl.when(home)
         def _():
-            for ka in range(2):
-                for e in (1, 3):
-                    to_near(ka, e, 0).wait_send()
-
-                @pl.when(k != ka)
-                def _():
-                    to_near(ka, 0, 0).wait_send()
+            five = rs.at[pl.ds(0, 5)]
+            remote(five, five, near_s.at[0], rs_r.at[0], sib).wait_send()
 
         @pl.when(away)
         def _():
-            for ka in range(2):
-                for e in (0, 1, 3):
-                    to_near(ka, e, 1).wait_send()
+            six = rs.at[pl.ds(0, 6)]
+            remote(six, six, near_s.at[0], rs_r.at[0], sib).wait_send()
 
 
 def on_device(factors, amplitudes, tile_mask):
@@ -498,7 +488,7 @@
             dma((1,)), dma((3,)), dma((2,)), dma((2,)), dma((2,)), dma((2,)),
             dma((1,)), dma((19,)), dma((1,)), dma((18,)), dma((1,)), dma((18,)),
             dma((1,)), dma((1,)), dma((1,)), dma((1,)),
-            dma((2, 2)), dma((2, 2)), dma((6,)), dma((6,)), dma((6,)), dma((9,)),
+            dma((1,)), dma((2, 2)), dma((1,)), dma((6,)), dma((1,)), dma((9,)),
         ],
         compiler_params=pltpu.CompilerParams(
             collective_id=0, has_side_effects=True, vmem_limit_bytes=VMEM_MIB * 1024 * 1024

time: 105 us -> 105 us (level)
  no operation moved by 1% of the time
where the time goes in v7:
time: 105 us
  Pallas kernels  101 us (96%)
  local copies, waits for them, and re-layouts  3.31 us (3%)
    pallas_call x1, Pallas kernels, on_device(): pl.pallas_call(kernel, name='ladder', out_shape=jax.ShapeDtypeStruct((256...  101 us
    transpose x1, local copies, waits for them, and re-layouts, on_device(): fl = factors.transpose(2, 1, 0).reshape(4, 4, 2, 2, 2, 32, 128)  2.59 us

profile of v7, /device:TPU:1, one launch (start us, length us, event | category | flops | bytes accessed | tf_op | source)
XLA Modules:
  0.0 104.7 jit_solution(13642436559663882756)
XLA Ops:
  0.0 0.0 copy-start
  0.0 0.0 copy-start.1
  0.0 0.0 copy-start.2
  0.0 2.6 %copy.4 = bf16[128,32,128]{2,1,0:T(8,128)(2,1)S(1)} copy(bf16[128,32,128]{0,1,2:T(8,128)(2,1)} %bitcast.4) | data formatting | bytes 2097152 | tf_op jit(solution)/shard_map/transpose | solution.py:465
  2.6 0.0 copy-done
  2.6 0.0 copy-done.1
  2.6 0.0 copy-done.2
  2.6 101.4 %ladder.1 = bf16[256,512]{1,0:T(8,128)(2,1)S(1)} custom-call(s32[2,2,32]{2,1,0:T(2,128)S(1)} %bitcast.7, bf16[4,4,2,2,2,32,128]{6,5,4,3,2,1,0:T(8,128)(2,1)S(1)} %bitcast.5, bf16[128,32,128]{2,1,0:T(8,128)(2,1)S(1)} %copy-done, bf16[64,32,128]{2,1,0:T(8,128)(2,1)S(1)} %copy-done.1), custom_call_target="tpu_custom_call" | custom-call | tf_op jit(solution)/shard_map/ladder/pallas_call | solution.py:468
  104.0 0.7 copy.6
Async XLA Ops:
  0.0 2.6 %copy-start = (bf16[128,32,128]{2,1,0:T(8,128)(2,1)S(1)}, bf16[128,32,128]{2,1,0:T(8,128)(2,1)}, u32[]{:S(2)}) copy-start(bf16[128,32,128]{2,1,0:T(8,128)(2,1)} %factors.1) | copy-start | bytes 3145732
  0.0 2.6 %copy-start.1 = (bf16[64,32,128]{2,1,0:T(8,128)(2,1)S(1)}, bf16[64,32,128]{2,1,0:T(8,128)(2,1)}, u32[]{:S(2)}) copy-start(bf16[64,32,128]{2,1,0:T(8,128)(2,1)} %amplitudes.1) | copy-start | bytes 1572868
  0.0 2.6 %copy-start.2 = (s32[32,2,2]{0,2,1:T(2,128)S(1)}, s32[32,2,2]{0,2,1:T(2,128)}, u32[]{:S(2)}) copy-start(s32[32,2,2]{0,2,1:T(2,128)} %param.5) | copy-start | bytes 1540
